TPU v7x, 128 devices: a whole 4x4x4 slice. The times are simulated.
128 devices in a mesh: section: 8 (over z_hi, x), state: 16 (over z_lo, y, core).
Axes of the slice: x: 4, y: 4, z: 4 (z_hi: 2, z_lo: 2; z = z_hi * 2 + z_lo), core: 2. Of those that a mesh axis runs over, the one named last changes fastest.
Arguments:
- belief: float32 [8, 512, 2048], P('section', None, 'state'), may hold values from 0 to 0.04
- action: int32 [8, 512], P('section'), may hold values from 0 to 7
- next_index: int32 [8, 512, 32], P('section'), may hold values from 0 to 511, as said below
- obs_table: float32 [8, 32, 2048], P(None, None, 'state'), may hold values from -1 to 1
- transition: bfloat16 [8, 2048, 2048], P(None, 'state'), may hold values from -0.1875 to 0.1875
- reward: float32 [8, 2048], P(None, 'state'), may hold values from -6 to 6
- terminal: float32 [512, 2048], P(None, 'state'), may hold values from -6 to 6
Outputs:
- alphas: float32 [8, 512, 2048], P('section', None, 'state')
- values: float32 [8, 512], P('section')
Inputs may be any that keep to these rules, and one draw needn't show every extreme that they name: next_index[h, b, o] < 128 * (b // 128 + 1): a belief of micro-batch m names only next-section alpha vectors of micro-batches 0 to m.
All inputs are finite; a program needn't handle non-finite values.
Results may differ from a plain program's by a relative error of at most 0.012.
Values sent between devices are 32-bit elements; how exact they have to be, the bound alone decides.
A program may use at most 64 MiB of HBM per device.

v0:
```python
import jax
import jax.numpy as jnp
from jax import lax
from jax.sharding import PartitionSpec as P

discount = 0.95


def cut_along(x, dim, peers):
    shape = x.shape
    blocks = x.reshape(*shape[:dim], peers, shape[dim] // peers, *shape[dim + 1 :])
    return jnp.moveaxis(blocks, dim, 0)


def sum_at_owner(x, axis, dim):
    blocks = cut_along(x, dim, lax.axis_size(axis))
    arrived = lax.all_to_all(blocks, axis, split_axis=0, concat_axis=0, tiled=True)
    return arrived.sum(axis=0)


def sent_to_all(x, axis):
    copies = jnp.broadcast_to(x, (lax.axis_size(axis), *x.shape))
    return lax.all_to_all(copies, axis, split_axis=0, concat_axis=0, tiled=True)


def over_copies(x, axis):
    return sent_to_all(x, axis).sum(axis=0)


def in_one_piece(arrays, axis, dim, along):
    columns = [a.reshape(*a.shape[:along], -1) for a in arrays]
    both = jnp.concatenate(columns, axis=along)
    result, at, done = (lax.all_gather(both, axis, axis=dim, tiled=True), 0, [])
    for a, column in zip(arrays, columns):
        piece = result[..., at : at + column.shape[along]]
        done.append(piece.reshape(*piece.shape[:along], *a.shape[along:]))
        at += column.shape[along]
    return tuple(done)


def in_order(blocks, dim):
    blocks = jnp.moveaxis(blocks, 0, dim)
    shape = blocks.shape
    return blocks.reshape(*shape[:dim], shape[dim] * shape[dim + 1], *shape[dim + 2 :])


def gathered_copies(x, axis, dim):
    return in_order(sent_to_all(x, axis), dim)


def in_one_piece_2(arrays, axis, split_dim, concat_dim, along):
    columns = [a.reshape(*a.shape[:along], -1) for a in arrays]
    both = jnp.concatenate(columns, axis=along)
    result, at, done = (
        lax.all_to_all(both, axis, split_axis=split_dim, concat_axis=concat_dim, tiled=True),
        0,
        [],
    )
    for a, column in zip(arrays, columns):
        piece = result[..., at : at + column.shape[along]]
        done.append(piece.reshape(*piece.shape[:along], *a.shape[along:]))
        at += column.shape[along]
    return tuple(done)


def backup(next_alphas, act_rows, next_rows, belief_rows, obs_table, transition, reward):
    actions = obs_table.shape[0]
    local_width = obs_table.shape[2]
    row_count = act_rows.shape[0]
    picked = next_alphas[next_rows]
    per_action = jnp.einsum("bos,aos->bas", picked, obs_table, precision=lax.Precision.HIGHEST)
    onehot = (act_rows[:, None] == jnp.arange(actions, dtype=jnp.int32)[None, :]).astype(
        jnp.float32
    )
    masked = (
        (per_action * onehot[:, :, None])
        .astype(jnp.bfloat16)
        .reshape(row_count, actions * local_width)
    )
    trans_flat = transition.reshape(actions * local_width, transition.shape[2])
    partial_value = jnp.dot(masked, trans_flat, preferred_element_type=jnp.float32)
    summed = sum_at_owner(partial_value, "state", 1)
    reward_rows = jnp.dot(onehot, reward, precision=lax.Precision.HIGHEST)
    section_alphas = reward_rows + discount * summed
    section_values = over_copies(jnp.sum(belief_rows * section_alphas, axis=1), "state")
    return (section_alphas, section_values)


def local(belief, action, next_index, obs_table, transition, reward, terminal):
    section_index = lax.axis_index("section")
    sections = lax.axis_size("section")
    beliefs = terminal.shape[0]
    local_width = terminal.shape[1]
    share = beliefs // sections
    every_action, every_next = in_one_piece((action, next_index), "section", 0, 2)
    shared_belief = lax.all_to_all(belief, "section", split_axis=1, concat_axis=0, tiled=True)
    offset = section_index * share

    def turn(turn_number, carry):
        nextset, kept_alphas, kept_values = carry
        horizon_step = (sections - 1 - turn_number).astype(jnp.int32)
        act_section = lax.dynamic_index_in_dim(every_action, horizon_step, 0, False)
        next_section_rows = lax.dynamic_index_in_dim(every_next, horizon_step, 0, False)
        act_rows = lax.dynamic_slice_in_dim(act_section, offset, share, 0)
        next_rows = lax.dynamic_slice_in_dim(next_section_rows, offset, share, 0)
        belief_rows = lax.dynamic_index_in_dim(shared_belief, horizon_step, 0, False)
        part_alphas, part_values = backup(
            nextset, act_rows, next_rows, belief_rows, obs_table, transition, reward
        )
        nextset = gathered_copies(part_alphas, "section", 0)
        kept_alphas = lax.dynamic_update_index_in_dim(kept_alphas, part_alphas, horizon_step, 0)
        kept_values = lax.dynamic_update_index_in_dim(kept_values, part_values, horizon_step, 0)
        return (nextset, kept_alphas, kept_values)

    start = (
        terminal,
        jnp.zeros((sections, share, local_width), jnp.float32),
        jnp.zeros((sections, share), jnp.float32),
    )
    result = lax.fori_loop(0, sections, turn, start)
    out_alphas, out_values = in_one_piece_2((result[1], result[2]), "section", 0, 1, 2)
    return (out_alphas, out_values)


def solution(mesh):
    return jax.shard_map(
        local,
        mesh=mesh,
        in_specs=(
            P("section", None, "state"),
            P("section", None),
            P("section", None, None),
            P(None, None, "state"),
            P(None, "state", None),
            P(None, "state"),
            P(None, "state"),
        ),
        out_specs=(P("section", None, "state"), P("section", None)),
        check_vma=False,
    )
```

profile of v0, /device:TPU:1, one launch (start us, length us, event | category | flops | bytes accessed | tf_op | source)
XLA Modules:
  0.0 496.4 jit_solution(5463378755439692102)
XLA Ops:
  1.5 8.2 %all-to-all-start.3 = ((f32[1,512,128]{2,0,1:T(1,128)}), f32[1,512,128]{2,0,1:T(1,128)}, u32[]{:S(2)}, u32[]{:S(2)}) async-start(f32[1,512,128]{2,0,1:T(1,128)} %bitcast.86), calls=%async_computation.3 | async-start | bytes 524288 | tf_op jit(solution)/shard_map/all_to_all | solution.py:96
  9.7 31.4 %all_gather.3 = s32[8,512,33]{1,2,0:T(8,128)S(1)} all-gather(s32[1,512,33]{1,2,0:T(8,128)S(1)} %pad_add_fusion), channel_id=1, replica_groups=mesh['section'=8,'state'=16] {'section'}, dimensions={0}, use_global_device_ids=true | all-gather | bytes 608256 | tf_op jit(solution)/shard_map/all_gather | solution.py:33
  41.9 1.9 copy.44
  43.8 6.8 %copy.45 = bf16[8,128,2048]{1,0,2:T(8,128)(2,1)} copy(bf16[8,128,2048]{2,1,0:T(8,128)(2,1)} %param.13) | data formatting | bytes 8388608 | tf_op jit(solution)/shard_map/while | solution.py:120
  50.7 431.2 %while.20 = (s32[]{:T(128)}, f32[512,128]{1,0:T(8,128)S(1)}, f32[8,64,128]{2,1,0:T(8,128)S(1)}, f32[8,64]{1,0:T(8,128)S(1)}, s32[8,512]{1,0:T(8,128)S(1)}, /*ind...) while((s32[]{:T(128)}, f32[512,128]{1,0:T(8,128)S(1)}, ...), condition=%wide.region_4.5_spmd, body=%wide.region_0.4_spmd.sunk | while | flops 294685056 | bytes 22235928 | solution.py:120
  51.8 5.5 %gather_fusion = f32[2048,128]{1,0:T(8,128)S(1)} fusion(f32[512,128]{1,0:T(8,128)S(1)} %get-tuple-element.487, s32[2048]{0:T(1024)S(1)} %broadcast_clamp_fusion.2), kind=kCustom, calls=%fused_computation.clone.1 | custom fusion | bytes 2105344 | tf_op jit(solution)/shard_map/while/body/eval_jaxpr/gather | solution.py:70
  57.3 1.9 copy.59
  59.2 3.0 fusion.24
  62.4 3.3 copy.61
  67.1 20.5 %all_to_all.68 = f32[16,64,128]{2,1,0:T(8,128)S(1)} all-to-all(f32[16,64,128]{2,1,0:T(8,128)S(1)} %convolution_bitcast_fusion.2), channel_id=1, replica_groups=mesh['section'=8,'state'=16] {'state'}, dimensions={0} | all-to-all | bytes 1048576 | tf_op jit(solution)/shard_map/while/body/eval_jaxpr/all_to_all | solution.py:17
  88.8 9.4 %all_to_all.69 = f32[16,1,64]{2,1,0:T(1,128)S(1)} all-to-all(f32[16,1,64]{2,1,0:T(1,128)S(1)} %broadcast_in_dim.63), channel_id=1, replica_groups=mesh['section'=8,'state'=16] {'state'}, dimensions={0} | all-to-all | bytes 8192 | tf_op jit(solution)/shard_map/while/body/eval_jaxpr/all_to_all | solution.py:23
  98.9 5.5 %all-to-all-start.1 = ((f32[8,64,128]{2,1,0:T(8,128)}), f32[8,64,128]{2,1,0:T(8,128)S(1)}, u32[]{:S(2)}, u32[]{:S(2)}) async-start(f32[8,64,128]{2,1,0:T(8,128)} %broadcast_in_dim.62), calls=%async_computation.1 | async-start | bytes 524288 | tf_op jit(solution)/shard_map/while/body/eval_jaxpr/all_to_all | solution.py:23
  104.5 7.7 %all-to-all-done.1 = f32[8,64,128]{2,1,0:T(8,128)S(1)} async-done(((f32[8,64,128]{2,1,0:T(8,128)}), f32[8,64,128]{2,1,0:T(8,128)S(1)}, u32[]{:S(2)}, u32[]{:S(2)}) %all-to-all-start.1) | async-done | bytes 262176 | tf_op jit(solution)/shard_map/while/body/eval_jaxpr/all_to_all | solution.py:23
  113.3 5.5 %gather_fusion = f32[2048,128]{1,0:T(8,128)S(1)} fusion(f32[512,128]{1,0:T(8,128)S(1)} %get-tuple-element.487, s32[2048]{0:T(1024)S(1)} %broadcast_clamp_fusion.2), kind=kCustom, calls=%fused_computation.clone.1 | custom fusion | bytes 2105344 | tf_op jit(solution)/shard_map/while/body/eval_jaxpr/gather | solution.py:70
  118.8 1.9 copy.59
  120.7 3.0 fusion.24
  123.9 3.3 copy.61
  128.6 14.0 %all_to_all.68 = f32[16,64,128]{2,1,0:T(8,128)S(1)} all-to-all(f32[16,64,128]{2,1,0:T(8,128)S(1)} %convolution_bitcast_fusion.2), channel_id=1, replica_groups=mesh['section'=8,'state'=16] {'state'}, dimensions={0} | all-to-all | bytes 1048576 | tf_op jit(solution)/shard_map/while/body/eval_jaxpr/all_to_all | solution.py:17
  143.8 9.4 %all_to_all.69 = f32[16,1,64]{2,1,0:T(1,128)S(1)} all-to-all(f32[16,1,64]{2,1,0:T(1,128)S(1)} %broadcast_in_dim.63), channel_id=1, replica_groups=mesh['section'=8,'state'=16] {'state'}, dimensions={0} | all-to-all | bytes 8192 | tf_op jit(solution)/shard_map/while/body/eval_jaxpr/all_to_all | solution.py:23
  153.9 3.4 all-to-all-start.1
  157.3 8.1 %all-to-all-done.1 = f32[8,64,128]{2,1,0:T(8,128)S(1)} async-done(((f32[8,64,128]{2,1,0:T(8,128)}), f32[8,64,128]{2,1,0:T(8,128)S(1)}, u32[]{:S(2)}, u32[]{:S(2)}) %all-to-all-start.1) | async-done | bytes 262176 | tf_op jit(solution)/shard_map/while/body/eval_jaxpr/all_to_all | solution.py:23
  166.5 5.5 %gather_fusion = f32[2048,128]{1,0:T(8,128)S(1)} fusion(f32[512,128]{1,0:T(8,128)S(1)} %get-tuple-element.487, s32[2048]{0:T(1024)S(1)} %broadcast_clamp_fusion.2), kind=kCustom, calls=%fused_computation.clone.1 | custom fusion | bytes 2105344 | tf_op jit(solution)/shard_map/while/body/eval_jaxpr/gather | solution.py:70
  173.8 3.0 fusion.24
  177.1 3.3 copy.61
  181.8 13.6 %all_to_all.68 = f32[16,64,128]{2,1,0:T(8,128)S(1)} all-to-all(f32[16,64,128]{2,1,0:T(8,128)S(1)} %convolution_bitcast_fusion.2), channel_id=1, replica_groups=mesh['section'=8,'state'=16] {'state'}, dimensions={0} | all-to-all | bytes 1048576 | tf_op jit(solution)/shard_map/while/body/eval_jaxpr/all_to_all | solution.py:17
  196.5 9.4 %all_to_all.69 = f32[16,1,64]{2,1,0:T(1,128)S(1)} all-to-all(f32[16,1,64]{2,1,0:T(1,128)S(1)} %broadcast_in_dim.63), channel_id=1, replica_groups=mesh['section'=8,'state'=16] {'state'}, dimensions={0} | all-to-all | bytes 8192 | tf_op jit(solution)/shard_map/while/body/eval_jaxpr/all_to_all | solution.py:23
  206.6 3.4 all-to-all-start.1
  210.1 8.1 %all-to-all-done.1 = f32[8,64,128]{2,1,0:T(8,128)S(1)} async-done(((f32[8,64,128]{2,1,0:T(8,128)}), f32[8,64,128]{2,1,0:T(8,128)S(1)}, u32[]{:S(2)}, u32[]{:S(2)}) %all-to-all-start.1) | async-done | bytes 262176 | tf_op jit(solution)/shard_map/while/body/eval_jaxpr/all_to_all | solution.py:23
  219.2 5.5 %gather_fusion = f32[2048,128]{1,0:T(8,128)S(1)} fusion(f32[512,128]{1,0:T(8,128)S(1)} %get-tuple-element.487, s32[2048]{0:T(1024)S(1)} %broadcast_clamp_fusion.2), kind=kCustom, calls=%fused_computation.clone.1 | custom fusion | bytes 2105344 | tf_op jit(solution)/shard_map/while/body/eval_jaxpr/gather | solution.py:70
  226.6 3.0 fusion.24
  229.8 3.3 copy.61
  234.5 13.6 %all_to_all.68 = f32[16,64,128]{2,1,0:T(8,128)S(1)} all-to-all(f32[16,64,128]{2,1,0:T(8,128)S(1)} %convolution_bitcast_fusion.2), channel_id=1, replica_groups=mesh['section'=8,'state'=16] {'state'}, dimensions={0} | all-to-all | bytes 1048576 | tf_op jit(solution)/shard_map/while/body/eval_jaxpr/all_to_all | solution.py:17
  249.2 9.4 %all_to_all.69 = f32[16,1,64]{2,1,0:T(1,128)S(1)} all-to-all(f32[16,1,64]{2,1,0:T(1,128)S(1)} %broadcast_in_dim.63), channel_id=1, replica_groups=mesh['section'=8,'state'=16] {'state'}, dimensions={0} | all-to-all | bytes 8192 | tf_op jit(solution)/shard_map/while/body/eval_jaxpr/all_to_all | solution.py:23
  259.4 3.4 all-to-all-start.1
  262.8 8.1 %all-to-all-done.1 = f32[8,64,128]{2,1,0:T(8,128)S(1)} async-done(((f32[8,64,128]{2,1,0:T(8,128)}), f32[8,64,128]{2,1,0:T(8,128)S(1)}, u32[]{:S(2)}, u32[]{:S(2)}) %all-to-all-start.1) | async-done | bytes 262176 | tf_op jit(solution)/shard_map/while/body/eval_jaxpr/all_to_all | solution.py:23
  272.0 5.5 %gather_fusion = f32[2048,128]{1,0:T(8,128)S(1)} fusion(f32[512,128]{1,0:T(8,128)S(1)} %get-tuple-element.487, s32[2048]{0:T(1024)S(1)} %broadcast_clamp_fusion.2), kind=kCustom, calls=%fused_computation.clone.1 | custom fusion | bytes 2105344 | tf_op jit(solution)/shard_map/while/body/eval_jaxpr/gather | solution.py:70
  279.3 3.0 fusion.24
  282.6 3.3 copy.61
  287.3 13.6 %all_to_all.68 = f32[16,64,128]{2,1,0:T(8,128)S(1)} all-to-all(f32[16,64,128]{2,1,0:T(8,128)S(1)} %convolution_bitcast_fusion.2), channel_id=1, replica_groups=mesh['section'=8,'state'=16] {'state'}, dimensions={0} | all-to-all | bytes 1048576 | tf_op jit(solution)/shard_map/while/body/eval_jaxpr/all_to_all | solution.py:17
  302.0 9.4 %all_to_all.69 = f32[16,1,64]{2,1,0:T(1,128)S(1)} all-to-all(f32[16,1,64]{2,1,0:T(1,128)S(1)} %broadcast_in_dim.63), channel_id=1, replica_groups=mesh['section'=8,'state'=16] {'state'}, dimensions={0} | all-to-all | bytes 8192 | tf_op jit(solution)/shard_map/while/body/eval_jaxpr/all_to_all | solution.py:23
  312.1 3.4 all-to-all-start.1
  315.6 8.1 %all-to-all-done.1 = f32[8,64,128]{2,1,0:T(8,128)S(1)} async-done(((f32[8,64,128]{2,1,0:T(8,128)}), f32[8,64,128]{2,1,0:T(8,128)S(1)}, u32[]{:S(2)}, u32[]{:S(2)}) %all-to-all-start.1) | async-done | bytes 262176 | tf_op jit(solution)/shard_map/while/body/eval_jaxpr/all_to_all | solution.py:23
  324.7 5.5 %gather_fusion = f32[2048,128]{1,0:T(8,128)S(1)} fusion(f32[512,128]{1,0:T(8,128)S(1)} %get-tuple-element.487, s32[2048]{0:T(1024)S(1)} %broadcast_clamp_fusion.2), kind=kCustom, calls=%fused_computation.clone.1 | custom fusion | bytes 2105344 | tf_op jit(solution)/shard_map/while/body/eval_jaxpr/gather | solution.py:70
  332.1 3.0 fusion.24
  335.3 3.3 copy.61
  340.0 13.6 %all_to_all.68 = f32[16,64,128]{2,1,0:T(8,128)S(1)} all-to-all(f32[16,64,128]{2,1,0:T(8,128)S(1)} %convolution_bitcast_fusion.2), channel_id=1, replica_groups=mesh['section'=8,'state'=16] {'state'}, dimensions={0} | all-to-all | bytes 1048576 | tf_op jit(solution)/shard_map/while/body/eval_jaxpr/all_to_all | solution.py:17
  354.7 9.4 %all_to_all.69 = f32[16,1,64]{2,1,0:T(1,128)S(1)} all-to-all(f32[16,1,64]{2,1,0:T(1,128)S(1)} %broadcast_in_dim.63), channel_id=1, replica_groups=mesh['section'=8,'state'=16] {'state'}, dimensions={0} | all-to-all | bytes 8192 | tf_op jit(solution)/shard_map/while/body/eval_jaxpr/all_to_all | solution.py:23
  364.9 3.4 all-to-all-start.1
  368.3 8.1 %all-to-all-done.1 = f32[8,64,128]{2,1,0:T(8,128)S(1)} async-done(((f32[8,64,128]{2,1,0:T(8,128)}), f32[8,64,128]{2,1,0:T(8,128)S(1)}, u32[]{:S(2)}, u32[]{:S(2)}) %all-to-all-start.1) | async-done | bytes 262176 | tf_op jit(solution)/shard_map/while/body/eval_jaxpr/all_to_all | solution.py:23
  377.5 5.5 %gather_fusion = f32[2048,128]{1,0:T(8,128)S(1)} fusion(f32[512,128]{1,0:T(8,128)S(1)} %get-tuple-element.487, s32[2048]{0:T(1024)S(1)} %broadcast_clamp_fusion.2), kind=kCustom, calls=%fused_computation.clone.1 | custom fusion | bytes 2105344 | tf_op jit(solution)/shard_map/while/body/eval_jaxpr/gather | solution.py:70
  384.8 3.0 fusion.24
  388.1 3.3 copy.61
  392.8 13.6 %all_to_all.68 = f32[16,64,128]{2,1,0:T(8,128)S(1)} all-to-all(f32[16,64,128]{2,1,0:T(8,128)S(1)} %convolution_bitcast_fusion.2), channel_id=1, replica_groups=mesh['section'=8,'state'=16] {'state'}, dimensions={0} | all-to-all | bytes 1048576 | tf_op jit(solution)/shard_map/while/body/eval_jaxpr/all_to_all | solution.py:17
  407.5 9.4 %all_to_all.69 = f32[16,1,64]{2,1,0:T(1,128)S(1)} all-to-all(f32[16,1,64]{2,1,0:T(1,128)S(1)} %broadcast_in_dim.63), channel_id=1, replica_groups=mesh['section'=8,'state'=16] {'state'}, dimensions={0} | all-to-all | bytes 8192 | tf_op jit(solution)/shard_map/while/body/eval_jaxpr/all_to_all | solution.py:23
  417.6 3.4 all-to-all-start.1
  421.1 8.1 %all-to-all-done.1 = f32[8,64,128]{2,1,0:T(8,128)S(1)} async-done(((f32[8,64,128]{2,1,0:T(8,128)}), f32[8,64,128]{2,1,0:T(8,128)S(1)}, u32[]{:S(2)}, u32[]{:S(2)}) %all-to-all-start.1) | async-done | bytes 262176 | tf_op jit(solution)/shard_map/while/body/eval_jaxpr/all_to_all | solution.py:23
  430.2 5.5 %gather_fusion = f32[2048,128]{1,0:T(8,128)S(1)} fusion(f32[512,128]{1,0:T(8,128)S(1)} %get-tuple-element.487, s32[2048]{0:T(1024)S(1)} %broadcast_clamp_fusion.2), kind=kCustom, calls=%fused_computation.clone.1 | custom fusion | bytes 2105344 | tf_op jit(solution)/shard_map/while/body/eval_jaxpr/gather | solution.py:70
  437.6 3.0 fusion.24
  440.8 3.3 copy.61
  445.5 13.6 %all_to_all.68 = f32[16,64,128]{2,1,0:T(8,128)S(1)} all-to-all(f32[16,64,128]{2,1,0:T(8,128)S(1)} %convolution_bitcast_fusion.2), channel_id=1, replica_groups=mesh['section'=8,'state'=16] {'state'}, dimensions={0} | all-to-all | bytes 1048576 | tf_op jit(solution)/shard_map/while/body/eval_jaxpr/all_to_all | solution.py:17
  460.2 9.4 %all_to_all.69 = f32[16,1,64]{2,1,0:T(1,128)S(1)} all-to-all(f32[16,1,64]{2,1,0:T(1,128)S(1)} %broadcast_in_dim.63), channel_id=1, replica_groups=mesh['section'=8,'state'=16] {'state'}, dimensions={0} | all-to-all | bytes 8192 | tf_op jit(solution)/shard_map/while/body/eval_jaxpr/all_to_all | solution.py:23
  470.4 3.4 all-to-all-start.1
  473.8 8.1 %all-to-all-done.1 = f32[8,64,128]{2,1,0:T(8,128)S(1)} async-done(((f32[8,64,128]{2,1,0:T(8,128)}), f32[8,64,128]{2,1,0:T(8,128)S(1)}, u32[]{:S(2)}, u32[]{:S(2)}) %all-to-all-start.1) | async-done | bytes 262176 | tf_op jit(solution)/shard_map/while/body/eval_jaxpr/all_to_all | solution.py:23
  482.1 12.9 %all_to_all.67 = f32[8,64,129]{2,1,0:T(8,128)S(1)} all-to-all(f32[8,64,129]{2,1,0:T(8,128)S(1)} %pad_maximum_fusion), channel_id=1, replica_groups=mesh['section'=8,'state'=16] {'section'}, dimensions={0} | all-to-all | bytes 528384 | tf_op jit(solution)/shard_map/all_to_all | solution.py:55
  (157 shorter events, 51.8 us)
Async XLA Ops:
  1.5 49.2 %all-to-all-start.3 = ((f32[1,512,128]{2,0,1:T(1,128)}), f32[1,512,128]{2,0,1:T(1,128)}, u32[]{:S(2)}, u32[]{:S(2)}) async-start(f32[1,512,128]{2,0,1:T(1,128)} %bitcast.86), calls=%async_computation.3 | async-start | bytes 524288 | tf_op jit(solution)/shard_map/all_to_all | solution.py:96
  43.8 6.9 %copy-start = (f32[512,128]{1,0:T(8,128)S(1)}, f32[512,128]{1,0:T(8,128)}, u32[]{:S(2)}) copy-start(f32[512,128]{1,0:T(8,128)} %param.15) | copy-start | bytes 786436
  43.8 6.9 %copy-start.1 = (f32[8,128]{1,0:T(8,128)S(1)}, f32[8,128]{1,0:T(8,128)}, u32[]{:S(2)}) copy-start(f32[8,128]{1,0:T(8,128)} %param.14) | copy-start | bytes 12292
  98.9 13.3 %all-to-all-start.1 = ((f32[8,64,128]{2,1,0:T(8,128)}), f32[8,64,128]{2,1,0:T(8,128)S(1)}, u32[]{:S(2)}, u32[]{:S(2)}) async-start(f32[8,64,128]{2,1,0:T(8,128)} %broadcast_in_dim.62), calls=%async_computation.1 | async-start | bytes 524288 | tf_op jit(solution)/shard_map/while/body/eval_jaxpr/all_to_all | solution.py:23
  153.9 11.5 %all-to-all-start.1 = ((f32[8,64,128]{2,1,0:T(8,128)}), f32[8,64,128]{2,1,0:T(8,128)S(1)}, u32[]{:S(2)}, u32[]{:S(2)}) async-start(f32[8,64,128]{2,1,0:T(8,128)} %broadcast_in_dim.62), calls=%async_computation.1 | async-start | bytes 524288 | tf_op jit(solution)/shard_map/while/body/eval_jaxpr/all_to_all | solution.py:23
  206.6 11.5 %all-to-all-start.1 = ((f32[8,64,128]{2,1,0:T(8,128)}), f32[8,64,128]{2,1,0:T(8,128)S(1)}, u32[]{:S(2)}, u32[]{:S(2)}) async-start(f32[8,64,128]{2,1,0:T(8,128)} %broadcast_in_dim.62), calls=%async_computation.1 | async-start | bytes 524288 | tf_op jit(solution)/shard_map/while/body/eval_jaxpr/all_to_all | solution.py:23
  259.4 11.5 %all-to-all-start.1 = ((f32[8,64,128]{2,1,0:T(8,128)}), f32[8,64,128]{2,1,0:T(8,128)S(1)}, u32[]{:S(2)}, u32[]{:S(2)}) async-start(f32[8,64,128]{2,1,0:T(8,128)} %broadcast_in_dim.62), calls=%async_computation.1 | async-start | bytes 524288 | tf_op jit(solution)/shard_map/while/body/eval_jaxpr/all_to_all | solution.py:23
  312.1 11.5 %all-to-all-start.1 = ((f32[8,64,128]{2,1,0:T(8,128)}), f32[8,64,128]{2,1,0:T(8,128)S(1)}, u32[]{:S(2)}, u32[]{:S(2)}) async-start(f32[8,64,128]{2,1,0:T(8,128)} %broadcast_in_dim.62), calls=%async_computation.1 | async-start | bytes 524288 | tf_op jit(solution)/shard_map/while/body/eval_jaxpr/all_to_all | solution.py:23
  364.9 11.5 %all-to-all-start.1 = ((f32[8,64,128]{2,1,0:T(8,128)}), f32[8,64,128]{2,1,0:T(8,128)S(1)}, u32[]{:S(2)}, u32[]{:S(2)}) async-start(f32[8,64,128]{2,1,0:T(8,128)} %broadcast_in_dim.62), calls=%async_computation.1 | async-start | bytes 524288 | tf_op jit(solution)/shard_map/while/body/eval_jaxpr/all_to_all | solution.py:23
  417.6 11.5 %all-to-all-start.1 = ((f32[8,64,128]{2,1,0:T(8,128)}), f32[8,64,128]{2,1,0:T(8,128)S(1)}, u32[]{:S(2)}, u32[]{:S(2)}) async-start(f32[8,64,128]{2,1,0:T(8,128)} %broadcast_in_dim.62), calls=%async_computation.1 | async-start | bytes 524288 | tf_op jit(solution)/shard_map/while/body/eval_jaxpr/all_to_all | solution.py:23
  470.4 11.5 %all-to-all-start.1 = ((f32[8,64,128]{2,1,0:T(8,128)}), f32[8,64,128]{2,1,0:T(8,128)S(1)}, u32[]{:S(2)}, u32[]{:S(2)}) async-start(f32[8,64,128]{2,1,0:T(8,128)} %broadcast_in_dim.62), calls=%async_computation.1 | async-start | bytes 524288 | tf_op jit(solution)/shard_map/while/body/eval_jaxpr/all_to_all | solution.py:23
where the time goes:
time: 501 us; the launch traced here: 496 us
  blocking collectives  235 us (47%)
  local copies, waits for them, and re-layouts  113 us (23%)
  waiting for transfers between devices  64.1 us (13%)
  starting transfers between devices  37.6 us (8%)
  matrix products  36.7 us (7%)
  other arithmetic  8.48 us (2%)
    all_to_all x8, blocking collectives, sum_at_owner(): lax.all_to_all(blocks, axis, split_axis=0, concat_axis=0, tiled=True)  116 us
    all_to_all x8, blocking collectives, sent_to_all(): return lax.all_to_all(copies, axis, split_axis=0, concat_axis=0, tiled=True)  75.1 us
    all_to_all x8, waiting for transfers between devices, sent_to_all(): return lax.all_to_all(copies, axis, split_axis=0, concat_axis=0, tiled=True)  64.1 us
    gather x16, local copies, waits for them, and re-layouts, backup(): picked = next_alphas[next_rows]  58.6 us
    all_gather x1, blocking collectives, in_one_piece(): result, at, done = (lax.all_gather(both, axis, axis=dim, tiled=True), 0, [])  31.4 us
    all_to_all x8, starting transfers between devices, sent_to_all(): return lax.all_to_all(copies, axis, split_axis=0, concat_axis=0, tiled=True)  29.4 us
    while x8, local copies, waits for them, and re-layouts  26.2 us
    dot_general x8, matrix products, backup(): jnp.einsum('bos,aos->bas', picked, obs_table, precision=lax.Precision.HIG...  23.8 us
  transfers between devices with their start and end apart: 9, of which 8 were waited for; matrix products, arithmetic and copies ran while one was open for 2% of the time, Pallas kernels for 0%

commit v1 on v0

v1 whole, which is shorter than its diff:
```python
import jax
import jax.numpy as jnp
from jax import lax
from jax.experimental import pallas as pl
from jax.experimental.pallas import tpu as pltpu
from jax.sharding import PartitionSpec as P

MESH = pl.DeviceIdType.MESH
discount = 0.95

ACTIONS = 8
OBS = 32
STEPS = 8
SECTIONS = 8
PLANES = 4
CHIPS = 8
SHARDS = 16
BELIEFS = 512
ROWS = 64
W = 128
GROUP = 8


def kernel(
    tab_ref, obs_ref, reward_ref, terminal_ref, trans_hbm, belief_hbm,
    alphas_ref, values_ref,
    trans, belief, nbuf, final, idx, onehot, weight, rewrow, masked,
    pair_send, pair_recv, part_send, part_recv, vbuf,
    load_sem, idx_ssem, idx_rsem, pair_ssem, pair_rsem, part_ssem, part_rsem,
    row_ssem, row_rsem, out_ssem, out_rsem, val_ssem, val_rsem,
):
    sec = lax.axis_index("section")
    st = lax.axis_index("state")
    plane, half = lax.rem(sec, PLANES), lax.div(sec, PLANES)
    core, chip = lax.rem(st, 2), lax.div(st, 2)
    my_chip_lo, my_chip_y = lax.div(chip, 4), lax.rem(chip, 4)

    def rows_of(s):
        return pl.ds(pl.multiple_of((lax.rem(s, PLANES) * 2 + lax.div(s, PLANES)) * ROWS, ROWS), ROWS)

    my_rows = rows_of(sec)

    trans_load = pltpu.make_async_copy(trans_hbm, trans, load_sem.at[0])
    trans_load.start()
    belief_load = pltpu.make_async_copy(belief_hbm, belief, load_sem.at[1])
    belief_load.start()

    def other_section(d):
        return lax.rem(sec + d, SECTIONS)

    def other_state(d):
        return lax.rem(st + d, SHARDS)

    @pl.loop(1, STEPS)
    def _(t):
        nbuf[t] = jnp.zeros((BELIEFS, W), jnp.float32)

    barrier = pltpu.get_barrier_semaphore()
    for d in range(1, SECTIONS):
        pl.semaphore_signal(barrier, inc=1, device_id={"section": other_section(d), "state": st}, device_id_type=MESH)
    for d in range(1, SHARDS):
        pl.semaphore_signal(barrier, inc=1, device_id={"section": sec, "state": other_state(d)}, device_id_type=MESH)
    pl.semaphore_wait(barrier, SECTIONS + SHARDS - 2)

    def idx_copy(d):
        to = other_section(d)
        return pltpu.make_async_remote_copy(
            src_ref=tab_ref.at[rows_of(to)], dst_ref=idx.at[sec],
            send_sem=idx_ssem.at[d], recv_sem=idx_rsem.at[sec],
            device_id={"section": to, "state": st}, device_id_type=MESH,
        )

    for d in range(1, SECTIONS):
        idx_copy(d).start()
    idx[pl.ds(sec, 1)] = tab_ref[my_rows][None]
    nbuf[0] = terminal_ref[...]

    def wait_idx(h):
        @pl.when(h != sec)
        def _():
            pltpu.make_async_remote_copy(
                src_ref=idx.at[h], dst_ref=idx.at[h], send_sem=idx_ssem.at[0], recv_sem=idx_rsem.at[h],
                device_id={"section": sec, "state": other_state(1)}, device_id_type=MESH,
            ).wait_recv()

    def prepare(t):
        h = STEPS - 1 - t
        wait_idx(h)
        table = idx[h]
        act = table[:, OBS : OBS + 1]
        row = jnp.zeros((ROWS, W), jnp.float32)
        for a in range(ACTIONS):
            row = jnp.where(act == a, reward_ref[a : a + 1, :], row)
        rewrow[...] = row
        wide = jnp.broadcast_to(act, (ROWS, W))
        column = lax.broadcasted_iota(jnp.int32, (ROWS, BELIEFS), 1)
        for o in range(OBS):
            pick = table[:, o : o + 1]
            onehot[o * ROWS : (o + 1) * ROWS, :] = (
                jnp.where(column == pick, 1.0, 0.0).astype(jnp.bfloat16)
            )
            w = jnp.zeros((ROWS, W), jnp.float32)
            for a in range(ACTIONS):
                w = jnp.where(wide == a, obs_ref[a, o : o + 1, :], w)
            weight[o] = w

    def chip_at(lo, y):
        return lax.rem(my_chip_lo + lo, 2) * 4 + lax.rem(my_chip_y + y, 4)

    order = ((1, 2), (0, 2), (1, 1), (1, 3), (0, 1), (0, 3), (1, 0), (0, 0))

    def pair_copy(k, t):
        return pltpu.make_async_remote_copy(
            src_ref=pair_send.at[k], dst_ref=pair_recv.at[t, k],
            send_sem=pair_ssem.at[k], recv_sem=pair_rsem.at[t, k],
            device_id={"section": sec, "state": chip * 2 + 1 - core}, device_id_type=MESH,
        )

    def part_copy(k, t):
        return pltpu.make_async_remote_copy(
            src_ref=part_send.at[k], dst_ref=part_recv.at[t, k],
            send_sem=part_ssem.at[k], recv_sem=part_rsem.at[t, k],
            device_id={"section": sec, "state": chip_at(*order[k]) * 2 + core}, device_id_type=MESH,
        )

    def row_copy(d, t):
        to = other_section(d)
        return pltpu.make_async_remote_copy(
            src_ref=nbuf.at[t + 1, my_rows], dst_ref=nbuf.at[t + 1, my_rows],
            send_sem=row_ssem.at[d], recv_sem=row_rsem.at[t, sec],
            device_id={"section": to, "state": st}, device_id_type=MESH,
        )

    def goes_to(d, t):
        to = other_section(d)
        p, f = lax.rem(to, PLANES), lax.div(to, PLANES)
        feeds = (p > plane) | ((p == plane) & (f != half))
        return feeds & (t < STEPS - 1)

    def out_copy(t):
        return pltpu.make_async_remote_copy(
            src_ref=nbuf.at[t + 1, my_rows], dst_ref=final.at[my_rows],
            send_sem=out_ssem, recv_sem=out_rsem.at[sec],
            device_id={"section": STEPS - 1 - t, "state": st}, device_id_type=MESH,
        )

    def wait_rows(source, t):
        pltpu.make_async_remote_copy(
            src_ref=nbuf.at[t + 1, rows_of(source)], dst_ref=nbuf.at[t + 1, rows_of(source)],
            send_sem=row_ssem.at[0], recv_sem=row_rsem.at[t, source],
            device_id={"section": source, "state": st}, device_id_type=MESH,
        ).wait_recv()

    def wait_sent(t):
        for d in range(1, SECTIONS):
            @pl.when(goes_to(d, t))
            def _():
                row_copy(d, t).wait_send()

        @pl.when(STEPS - 1 - t != sec)
        def _():
            out_copy(t).wait_send()

    prepare(0)
    trans_load.wait()

    def step(t, carry):
        following = nbuf[t]
        high = following.astype(jnp.bfloat16)
        low = (following - high.astype(jnp.float32)).astype(jnp.bfloat16)
        both = jnp.concatenate([high, low], axis=1)
        total = jnp.zeros((ROWS, W), jnp.float32)
        for c in range(OBS // GROUP):
            got = jnp.dot(
                onehot[c * GROUP * ROWS : (c + 1) * GROUP * ROWS, :], both,
                preferred_element_type=jnp.float32,
            )
            got = (got[:, :W] + got[:, W:]).reshape(GROUP, ROWS, W)
            total = total + jnp.sum(got * weight[c * GROUP : (c + 1) * GROUP], axis=0)
        act = idx[STEPS - 1 - t][:, OBS : OBS + 1]
        for a in range(ACTIONS):
            masked[:, a * W : (a + 1) * W] = jnp.where(act == a, total, 0.0).astype(jnp.bfloat16)

        mine = []
        for k in range(CHIPS):
            q = chip_at(*order[k])
            part = jnp.dot(
                masked[...], trans[:, pl.ds(pl.multiple_of(q * 2 * W, 2 * W), 2 * W)],
                preferred_element_type=jnp.float32,
            )
            pair_send[k] = jnp.where(core == 0, part[:, W:], part[:, :W])
            pair_copy(k, t).start()
            part_send[k] = jnp.where(core == 0, part[:, :W], part[:, W:])
        for k in range(CHIPS):
            pair_copy(k, t).wait_recv()
            part_send[k] = part_send[k] + pair_recv[t, k]
            if k < CHIPS - 1:
                part_copy(k, t).start()

        reward_part = rewrow[...]

        @pl.when(t < STEPS - 1)
        def _():
            prepare(t + 1)

        summed = part_send[CHIPS - 1]
        for k in range(CHIPS - 1):
            part_copy(k, t).wait_recv()
            summed = summed + part_recv[t, k]
        for k in range(CHIPS):
            pair_copy(k, t).wait_send()

        @pl.when(t > 0)
        def _():
            wait_sent(t - 1)

        fresh = reward_part + discount * summed
        nbuf[t + 1, my_rows] = fresh
        for d in range(1, SECTIONS):
            @pl.when(goes_to(d, t))
            def _():
                row_copy(d, t).start()

        @pl.when(STEPS - 1 - t != sec)
        def _():
            out_copy(t).start()

        @pl.when(STEPS - 1 - t == sec)
        def _():
            final[my_rows] = fresh

        for k in range(CHIPS - 1):
            part_copy(k, t).wait_send()

        @pl.when(t < STEPS - 1)
        def _():
            for d in range(1, SECTIONS):
                source = other_section(d)
                p, f = lax.rem(source, PLANES), lax.div(source, PLANES)

                @pl.when((p < plane) | ((p == plane) & (f != half)))
                def _():
                    wait_rows(source, t)

        return carry

    lax.fori_loop(0, STEPS, step, 0)

    for d in range(1, SECTIONS):
        source = other_section(d)
        pltpu.make_async_remote_copy(
            src_ref=final.at[rows_of(source)], dst_ref=final.at[rows_of(source)],
            send_sem=out_ssem, recv_sem=out_rsem.at[source],
            device_id={"section": source, "state": st}, device_id_type=MESH,
        ).wait_recv()

    belief_load.wait()
    alphas_ref[...] = final[...]
    product = final[...] * belief[...]
    for g in range(BELIEFS // W):
        block = product[g * W : (g + 1) * W, :].T
        vbuf[pl.ds(st, 1), g : g + 1, :] = jnp.sum(block, axis=0, keepdims=True)[None]

    def val_copy(d):
        return pltpu.make_async_remote_copy(
            src_ref=vbuf.at[st], dst_ref=vbuf.at[st],
            send_sem=val_ssem.at[d], recv_sem=val_rsem.at[d],
            device_id={"section": sec, "state": other_state(d)}, device_id_type=MESH,
        )

    for d in range(1, SHARDS):
        val_copy(d).start()
    wait_sent(STEPS - 1)
    for d in range(1, SECTIONS):
        idx_copy(d).wait_send()
    for d in range(1, SHARDS):
        val_copy(d).wait_recv()
    value = vbuf[0]
    for s in range(1, SHARDS):
        value = value + vbuf[s]
    values_ref[...] = value
    for d in range(1, SHARDS):
        val_copy(d).wait_send()


def local(belief, action, next_index, obs_table, transition, reward, terminal):
    table = jnp.concatenate([next_index[0], action[0][:, None]], axis=1)
    table = jnp.pad(table, ((0, 0), (0, W - OBS - 1)))
    vmem = pl.BlockSpec(memory_space=pltpu.VMEM)
    anywhere = pl.BlockSpec(memory_space=pl.ANY)
    dma = pltpu.SemaphoreType.DMA
    alphas, values = pl.pallas_call(
        kernel,
        out_shape=(
            jax.ShapeDtypeStruct((BELIEFS, W), jnp.float32),
            jax.ShapeDtypeStruct((BELIEFS // W, W), jnp.float32),
        ),
        in_specs=[vmem, vmem, vmem, vmem, anywhere, anywhere],
        out_specs=(vmem, vmem),
        scratch_shapes=[
            pltpu.VMEM((ACTIONS * W, SHARDS * W), jnp.bfloat16),
            pltpu.VMEM((BELIEFS, W), jnp.float32),
            pltpu.VMEM((STEPS + 1, BELIEFS, W), jnp.float32),
            pltpu.VMEM((BELIEFS, W), jnp.float32),
            pltpu.VMEM((SECTIONS, ROWS, W), jnp.int32),
            pltpu.VMEM((OBS * ROWS, BELIEFS), jnp.bfloat16),
            pltpu.VMEM((OBS, ROWS, W), jnp.float32),
            pltpu.VMEM((ROWS, W), jnp.float32),
            pltpu.VMEM((ROWS, ACTIONS * W), jnp.bfloat16),
            pltpu.VMEM((CHIPS, ROWS, W), jnp.float32),
            pltpu.VMEM((STEPS, CHIPS, ROWS, W), jnp.float32),
            pltpu.VMEM((CHIPS, ROWS, W), jnp.float32),
            pltpu.VMEM((STEPS, CHIPS, ROWS, W), jnp.float32),
            pltpu.VMEM((SHARDS, BELIEFS // W, W), jnp.float32),
            dma((2,)),
            dma((SECTIONS,)),
            dma((SECTIONS,)),
            dma((CHIPS,)),
            dma((STEPS, CHIPS)),
            dma((CHIPS,)),
            dma((STEPS, CHIPS)),
            dma((SECTIONS,)),
            dma((STEPS, SECTIONS)),
            dma,
            dma((SECTIONS,)),
            dma((SHARDS,)),
            dma((SHARDS,)),
        ],
        compiler_params=pltpu.CompilerParams(
            collective_id=0, has_side_effects=True, vmem_limit_bytes=60 * 1024 * 1024
        ),
        name="chain",
    )(
        table, obs_table, reward, terminal,
        transition.reshape(ACTIONS * W, SHARDS * W), belief[0],
    )
    return alphas[None], values.reshape(1, BELIEFS)


def solution(mesh):
    return jax.shard_map(
        local,
        mesh=mesh,
        in_specs=(
            P("section", None, "state"),
            P("section", None),
            P("section", None, None),
            P(None, None, "state"),
            P(None, "state", None),
            P(None, "state"),
            P(None, "state"),
        ),
        out_specs=(P("section", None, "state"), P("section", None)),
        check_vma=False,
    )
```

time: 501 us -> 138 us (0.28)
  blocking collectives: 235 us -> 0 us
  Pallas kernels: 0 us -> 132 us
  local copies, waits for them, and re-layouts: 113 us -> 3.78 us
  waiting for transfers between devices: 64.1 us -> 0 us
  starting transfers between devices: 37.6 us -> 0 us
  matrix products: 36.7 us -> 0 us
  other arithmetic: 8.48 us -> 0.86 us
    all_to_all x17 -> x0, blocking collectives: 204 us -> none  [the longest x8 116 us: sum_at_owner(): lax.all_to_all(blocks, axis, split_axis=0, concat_axis=0, tiled=True)]
    pallas_call x0 -> x1, Pallas kernels: none -> 132 us  [local(): pl.pallas_call(kernel, out_shape=(jax.ShapeDtypeStruct((BELIEFS, W), jnp....]
    all_to_all x9 -> x0, waiting for transfers between devices: 64.1 us -> none  [the longest x8 64.1 us: sent_to_all(): return lax.all_to_all(copies, axis, split_axis=0, concat_axis=0, tiled=True)]
    gather x16 -> x0, local copies, waits for them, and re-layouts: 58.6 us -> none  [backup(): picked = next_alphas[next_rows]]
    all_to_all x9 -> x0, starting transfers between devices: 37.6 us -> none  [the longest x8 29.4 us: sent_to_all(): return lax.all_to_all(copies, axis, split_axis=0, concat_axis=0, tiled=True)]
    dot_general x24 -> x0, matrix products: 36.7 us -> none  [the longest x8 23.8 us: backup(): jnp.einsum('bos,aos->bas', picked, obs_table, precision=lax.Precision.HIG...]
    while x10 -> x0, local copies, waits for them, and re-layouts: 35 us -> none
    all_gather x1 -> x0, blocking collectives: 31.4 us -> none  [in_one_piece(): result, at, done = (lax.all_gather(both, axis, axis=dim, tiled=True), 0, [])]
  transfers between devices with their start and end apart: 9 -> 0, of which waited for: 8 -> 0; matrix products, arithmetic and copies ran while one was open for 2% -> 0% of each run, Pallas kernels for 0% -> 0%
where the time goes in v1:
time: 138 us
  Pallas kernels  132 us (96%)
  local copies, waits for them, and re-layouts  3.78 us (3%)
    pallas_call x1, Pallas kernels, local(): pl.pallas_call(kernel, out_shape=(jax.ShapeDtypeStruct((BELIEFS, W), jnp....  132 us
    unnamed x2, local copies, waits for them, and re-layouts  2.92 us

profile of v1, /device:TPU:1, one launch (start us, length us, event | category | flops | bytes accessed | tf_op | source)
XLA Modules:
  0.0 137.6 jit_solution(6802939022033241284)
XLA Ops:
  0.6 0.9 pad_add_fusion
  1.5 0.1 copy.12
  1.6 0.7 pad.4.tab_ref
  2.4 132.3 %chain.1 = (f32[512,128]{1,0:T(8,128)}, f32[4,128]{1,0:T(4,128)}) custom-call(s32[512,128]{1,0:T(8,128)} %pad.4.tab_ref, f32[8,32,128]{2,1,0:T(8,128)} %obs_ref.1, f32[8,128]{1,0:T(8,128)} %reward_ref.1, f32[512,128]{1,0:T(8,128)} %terminal_ref.1, bf16[1024,2048]{1,0:T(8,128)(2,1)} %bitcast.6, f32[512,128]{1,0:T(8,128)} %bitcast.7), custom_call_target="tpu_custom_call" | custom-call | tf_op jit(solution)/shard_map/chain/pallas_call | solution.py:292
  134.7 1.7 %copy.15 = f32[1,512,128]{2,1,0:T(8,128)} copy(f32[1,512,128]{2,1,0:T(8,128)} %bitcast.8) | data formatting | bytes 524288
  136.4 1.2 copy.16

commit v2 on v1

v2 whole, which is shorter than its diff:
```python
import jax
import jax.numpy as jnp
from jax import lax
from jax.experimental import pallas as pl
from jax.experimental.pallas import tpu as pltpu
from jax.sharding import PartitionSpec as P

MESH = pl.DeviceIdType.MESH
discount = 0.95

ACTIONS = 8
OBS = 32
STEPS = 8
SECTIONS = 8
PLANES = 4
CHIPS = 8
SHARDS = 16
BELIEFS = 512
BATCH = 128
ROWS = 64
W = 128
TAB = 40
GROUP = 8


def kernel(
    next_ref, action_ref, reward_ref, obs_hbm, terminal_hbm, trans_hbm, belief_hbm,
    final, vbuf,
    obs, trans, belief, nbuf, tab, idx, turned, onehot, weight, rewrow, masked,
    pair_send, pair_recv, part_send, part_recv, sums_send, sums,
    load_sem, idx_ssem, idx_rsem, pair_ssem, pair_rsem, part_ssem, part_rsem,
    sums_ssem, sums_rsem, row_ssem, row_rsem, out_ssem, out_rsem, val_ssem, val_rsem,
):
    sec = lax.axis_index("section")
    st = lax.axis_index("state")
    plane, half = lax.rem(sec, PLANES), lax.div(sec, PLANES)
    core, chip = lax.rem(st, 2), lax.div(st, 2)
    lo, y = lax.div(chip, 4), lax.rem(chip, 4)

    def rows_of(p):
        return pl.ds(pl.multiple_of(p * BATCH, BATCH), BATCH)

    def other_section(d):
        return lax.rem(sec + d, SECTIONS)

    def other_state(d):
        return lax.rem(st + d, SHARDS)

    def other_plane(d):
        return lax.rem(plane + d, PLANES)

    def z_neighbour(up):
        z = lax.rem(half * 2 + lo + (1 if up else 3), 4)
        return {"section": lax.div(z, 2) * PLANES + plane, "state": (lax.rem(z, 2) * 4 + y) * 2 + core}

    loads = [
        pltpu.make_async_copy(obs_hbm, obs, load_sem.at[0]),
        pltpu.make_async_copy(terminal_hbm, nbuf.at[0], load_sem.at[1]),
        pltpu.make_async_copy(trans_hbm, trans, load_sem.at[2]),
        pltpu.make_async_copy(belief_hbm, belief, load_sem.at[3]),
    ]
    for load in loads:
        load.start()

    barrier = pltpu.get_barrier_semaphore()
    for d in range(1, SECTIONS):
        pl.semaphore_signal(barrier, inc=1, device_id={"section": other_section(d), "state": st}, device_id_type=MESH)
    for d in range(1, SHARDS):
        pl.semaphore_signal(barrier, inc=1, device_id={"section": sec, "state": other_state(d)}, device_id_type=MESH)
    for up in (True, False):
        pl.semaphore_signal(barrier, inc=1, device_id=z_neighbour(up), device_id_type=MESH)

    for p in range(PLANES):
        tab[p, 0:OBS, :] = next_ref[:, p * BATCH : (p + 1) * BATCH]
        tab[p, OBS : OBS + 1, :] = action_ref[:, p * BATCH : (p + 1) * BATCH]
        tab[p, OBS + 1 :, :] = jnp.zeros((TAB - OBS - 1, BATCH), jnp.int32)
        for t in range(1, STEPS):
            @pl.when(p > plane)
            def _():
                nbuf[t, p * BATCH : (p + 1) * BATCH, :] = jnp.zeros((BATCH, W), jnp.float32)
    idx[pl.ds(sec, 1)] = tab[pl.ds(plane, 1)]

    pl.semaphore_wait(barrier, SECTIONS + SHARDS)

    def idx_copy(d):
        to = other_section(d)
        return pltpu.make_async_remote_copy(
            src_ref=tab.at[lax.rem(to, PLANES)], dst_ref=idx.at[sec],
            send_sem=idx_ssem.at[d], recv_sem=idx_rsem.at[sec],
            device_id={"section": to, "state": st}, device_id_type=MESH,
        )

    for d in range(1, SECTIONS):
        idx_copy(d).start()

    def prepare(t):
        h = STEPS - 1 - t

        @pl.when(h != sec)
        def _():
            pltpu.make_async_remote_copy(
                src_ref=idx.at[h], dst_ref=idx.at[h], send_sem=idx_ssem.at[0], recv_sem=idx_rsem.at[h],
                device_id={"section": sec, "state": other_state(1)}, device_id_type=MESH,
            ).wait_recv()

        turned[...] = idx[h].T
        act = turned[:, OBS : OBS + 1]
        row = jnp.zeros((BATCH, W), jnp.float32)
        for a in range(ACTIONS):
            row = jnp.where(act == a, reward_ref[a : a + 1, :], row)
        rewrow[lax.rem(t, 2)] = row
        table = turned[pl.ds(pl.multiple_of(half * ROWS, ROWS), ROWS), :]
        wide = jnp.broadcast_to(table[:, OBS : OBS + 1], (ROWS, W))
        column = lax.broadcasted_iota(jnp.int32, (ROWS, BELIEFS), 1)
        for o in range(OBS):
            pick = table[:, o : o + 1]
            onehot[o * ROWS : (o + 1) * ROWS, :] = (
                jnp.where(column == pick, 1.0, 0.0).astype(jnp.bfloat16)
            )
            w = jnp.zeros((ROWS, W), jnp.float32)
            for a in range(ACTIONS):
                w = jnp.where(wide == a, obs[a, o : o + 1, :], w)
            weight[o] = w

    order = ((1, 2), (0, 2), (1, 1), (1, 3), (0, 1), (0, 3), (1, 0), (0, 0))

    def chip_at(k, flip):
        return lax.rem(lo + order[k][0] + flip, 2) * 4 + lax.rem(y + order[k][1], 4)

    def pair_copy(k, t):
        return pltpu.make_async_remote_copy(
            src_ref=pair_send.at[k], dst_ref=pair_recv.at[t, k],
            send_sem=pair_ssem.at[k], recv_sem=pair_rsem.at[t, k],
            device_id={"section": sec, "state": chip * 2 + 1 - core}, device_id_type=MESH,
        )

    def part_copy(k, t):
        return pltpu.make_async_remote_copy(
            src_ref=part_send.at[k], dst_ref=part_recv.at[t, k],
            send_sem=part_ssem.at[k], recv_sem=part_rsem.at[t, k],
            device_id={"section": sec, "state": chip_at(k, 0) * 2 + core}, device_id_type=MESH,
        )

    def sums_copy(up, t):
        return pltpu.make_async_remote_copy(
            src_ref=sums_send, dst_ref=sums.at[t, half],
            send_sem=sums_ssem.at[int(up)], recv_sem=sums_rsem.at[t, half],
            device_id=z_neighbour(up), device_id_type=MESH,
        )

    def wait_sums(f, t):
        pltpu.make_async_remote_copy(
            src_ref=sums_send, dst_ref=sums.at[t, f],
            send_sem=sums_ssem.at[0], recv_sem=sums_rsem.at[t, f],
            device_id=z_neighbour(True), device_id_type=MESH,
        ).wait_recv()

    def row_copy(d, t):
        return pltpu.make_async_remote_copy(
            src_ref=nbuf.at[t + 1, rows_of(plane)], dst_ref=nbuf.at[t + 1, rows_of(plane)],
            send_sem=row_ssem.at[d], recv_sem=row_rsem.at[t, plane],
            device_id={"section": half * PLANES + other_plane(d), "state": st}, device_id_type=MESH,
        )

    def feeds(d, t):
        return (other_plane(d) > plane) & (t < STEPS - 1)

    def wait_rows(p, t):
        pltpu.make_async_remote_copy(
            src_ref=nbuf.at[t + 1, rows_of(p)], dst_ref=nbuf.at[t + 1, rows_of(p)],
            send_sem=row_ssem.at[0], recv_sem=row_rsem.at[t, p],
            device_id={"section": half * PLANES + other_plane(1), "state": st}, device_id_type=MESH,
        ).wait_recv()

    def out_copy(t):
        return pltpu.make_async_remote_copy(
            src_ref=nbuf.at[t + 1, rows_of(plane)], dst_ref=final.at[rows_of(plane)],
            send_sem=out_ssem, recv_sem=out_rsem.at[plane],
            device_id={"section": STEPS - 1 - t, "state": st}, device_id_type=MESH,
        )

    def goes_out(t):
        owner = STEPS - 1 - t
        return (lax.div(owner, PLANES) == half) & (lax.rem(owner, PLANES) < plane)

    def wait_sent(t):
        for d in range(1, PLANES):
            @pl.when(feeds(d, t))
            def _():
                row_copy(d, t).wait_send()

        @pl.when(goes_out(t))
        def _():
            out_copy(t).wait_send()

    loads[0].wait()
    prepare(0)
    loads[1].wait()
    loads[2].wait()

    def step(t, carry):
        following = nbuf[t]
        high = following.astype(jnp.bfloat16)
        low = (following - high.astype(jnp.float32)).astype(jnp.bfloat16)
        both = jnp.concatenate([high, low], axis=1)
        total = jnp.zeros((ROWS, W), jnp.float32)
        for c in range(OBS // GROUP):
            got = jnp.dot(
                onehot[c * GROUP * ROWS : (c + 1) * GROUP * ROWS, :], both,
                preferred_element_type=jnp.float32,
            )
            got = (got[:, :W] + got[:, W:]).reshape(GROUP, ROWS, W)
            total = total + jnp.sum(got * weight[c * GROUP : (c + 1) * GROUP], axis=0)
        act = turned[pl.ds(pl.multiple_of(half * ROWS, ROWS), ROWS), :][:, OBS : OBS + 1]
        for a in range(ACTIONS):
            masked[:, a * W : (a + 1) * W] = jnp.where(act == a, total, 0.0).astype(jnp.bfloat16)

        for k in range(CHIPS):
            part = jnp.dot(
                masked[...], trans[:, pl.ds(pl.multiple_of(chip_at(k, 1) * 2 * W, 2 * W), 2 * W)],
                preferred_element_type=jnp.float32,
            )
            pair_send[k] = jnp.where(core == 0, part[:, W:], part[:, :W])
            pair_copy(k, t).start()
            part_send[k] = jnp.where(core == 0, part[:, :W], part[:, W:])
        for k in range(CHIPS):
            pair_copy(k, t).wait_recv()
            part_send[k] = part_send[k] + pair_recv[t, k]
            if k < CHIPS - 1:
                part_copy(k, t).start()

        @pl.when(t > 0)
        def _():
            wait_sent(t - 1)

        @pl.when(t < STEPS - 1)
        def _():
            prepare(t + 1)

        for k in range(CHIPS):
            pair_copy(k, t).wait_send()
        summed = part_send[CHIPS - 1]
        for k in range(CHIPS - 1):
            part_copy(k, t).wait_recv()
            summed = summed + part_recv[t, k]
        sums_send[...] = summed
        for up in (True, False):
            sums_copy(up, t).start()
        for k in range(CHIPS - 1):
            part_copy(k, t).wait_send()
        for f in (0, 1):
            wait_sums(f, t)
        nbuf[t + 1, rows_of(plane)] = (
            rewrow[lax.rem(t, 2)] + discount * sums[t].reshape(BATCH, W)
        )
        for d in range(1, PLANES):
            @pl.when(feeds(d, t))
            def _():
                row_copy(d, t).start()

        @pl.when(goes_out(t))
        def _():
            out_copy(t).start()

        for up in (True, False):
            sums_copy(up, t).wait_send()

        @pl.when(t < STEPS - 1)
        def _():
            for p in range(PLANES - 1):
                @pl.when(p < plane)
                def _():
                    wait_rows(p, t)

        return carry

    lax.fori_loop(0, STEPS, step, 0)

    own = STEPS - 1 - sec
    for p in range(PLANES):
        @pl.when(p <= plane)
        def _():
            final[p * BATCH : (p + 1) * BATCH, :] = nbuf[own + 1, p * BATCH : (p + 1) * BATCH, :]

    loads[3].wait()
    for p in range(PLANES):
        @pl.when(p > plane)
        def _():
            pltpu.make_async_remote_copy(
                src_ref=final.at[rows_of(p)], dst_ref=final.at[rows_of(p)],
                send_sem=out_ssem, recv_sem=out_rsem.at[p],
                device_id={"section": half * PLANES + other_plane(1), "state": st}, device_id_type=MESH,
            ).wait_recv()

        block = final[p * BATCH : (p + 1) * BATCH, :] * belief[p * BATCH : (p + 1) * BATCH, :]
        vbuf[pl.ds(st, 1), p : p + 1, :] = jnp.sum(block.T, axis=0, keepdims=True)[None]

    def val_copy(d):
        return pltpu.make_async_remote_copy(
            src_ref=vbuf.at[st], dst_ref=vbuf.at[st],
            send_sem=val_ssem.at[d], recv_sem=val_rsem.at[d],
            device_id={"section": sec, "state": other_state(d)}, device_id_type=MESH,
        )

    for d in range(1, SHARDS):
        val_copy(d).start()
    wait_sent(STEPS - 1)
    for d in range(1, SECTIONS):
        idx_copy(d).wait_send()
    for d in range(1, SHARDS):
        val_copy(d).wait_recv()
    for d in range(1, SHARDS):
        val_copy(d).wait_send()


def finish(final_ref, vbuf_ref, alphas_ref, values_ref):
    alphas_ref[...] = final_ref[...]
    value = vbuf_ref[0]
    for s in range(1, SHARDS):
        value = value + vbuf_ref[s]
    values_ref[...] = value


def local(belief, action, next_index, obs_table, transition, reward, terminal):
    vmem = pl.BlockSpec(memory_space=pltpu.VMEM)
    anywhere = pl.BlockSpec(memory_space=pl.ANY)
    dma = pltpu.SemaphoreType.DMA
    f32 = jnp.float32
    final, parts = pl.pallas_call(
        kernel,
        out_shape=(
            jax.ShapeDtypeStruct((BELIEFS, W), f32),
            jax.ShapeDtypeStruct((SHARDS, PLANES, W), f32),
        ),
        in_specs=[vmem, vmem, vmem, anywhere, anywhere, anywhere, anywhere],
        out_specs=(vmem, vmem),
        scratch_shapes=[
            pltpu.VMEM((ACTIONS, OBS, W), f32),
            pltpu.VMEM((ACTIONS * W, SHARDS * W), jnp.bfloat16),
            pltpu.VMEM((BELIEFS, W), f32),
            pltpu.VMEM((STEPS + 1, BELIEFS, W), f32),
            pltpu.VMEM((PLANES, TAB, BATCH), jnp.int32),
            pltpu.VMEM((SECTIONS, TAB, BATCH), jnp.int32),
            pltpu.VMEM((BATCH, TAB), jnp.int32),
            pltpu.VMEM((OBS * ROWS, BELIEFS), jnp.bfloat16),
            pltpu.VMEM((OBS, ROWS, W), f32),
            pltpu.VMEM((2, BATCH, W), f32),
            pltpu.VMEM((ROWS, ACTIONS * W), jnp.bfloat16),
            pltpu.VMEM((CHIPS, ROWS, W), f32),
            pltpu.VMEM((STEPS, CHIPS, ROWS, W), f32),
            pltpu.VMEM((CHIPS, ROWS, W), f32),
            pltpu.VMEM((STEPS, CHIPS, ROWS, W), f32),
            pltpu.VMEM((ROWS, W), f32),
            pltpu.VMEM((STEPS, 2, ROWS, W), f32),
            dma((4,)),
            dma((SECTIONS,)),
            dma((SECTIONS,)),
            dma((CHIPS,)),
            dma((STEPS, CHIPS)),
            dma((CHIPS,)),
            dma((STEPS, CHIPS)),
            dma((2,)),
            dma((STEPS, 2)),
            dma((PLANES,)),
            dma((STEPS, PLANES)),
            dma,
            dma((PLANES,)),
            dma((SHARDS,)),
            dma((SHARDS,)),
        ],
        compiler_params=pltpu.CompilerParams(
            collective_id=0, has_side_effects=True, vmem_limit_bytes=60 * 1024 * 1024
        ),
        name="chain",
    )(
        next_index[0].T, action, reward, obs_table, terminal,
        transition.reshape(ACTIONS * W, SHARDS * W), belief[0],
    )
    alphas, values = pl.pallas_call(
        finish,
        out_shape=(
            jax.ShapeDtypeStruct((BELIEFS, W), f32),
            jax.ShapeDtypeStruct((PLANES, W), f32),
        ),
        in_specs=[vmem, vmem],
        out_specs=(vmem, vmem),
        name="finish",
    )(final, parts)
    return alphas[None], values.reshape(1, BELIEFS)


def solution(mesh):
    return jax.shard_map(
        local,
        mesh=mesh,
        in_specs=(
            P("section", None, "state"),
            P("section", None),
            P("section", None, None),
            P(None, None, "state"),
            P(None, "state", None),
            P(None, "state"),
            P(None, "state"),
        ),
        out_specs=(P("section", None, "state"), P("section", None)),
        check_vma=False,
    )
```

time: 138 us -> 128 us (0.928)
  Pallas kernels: 132 us -> 127 us
  local copies, waits for them, and re-layouts: 3.78 us -> 0 us
    pallas_call x1 -> x2, Pallas kernels: 132 us -> 127 us  [the longest x1 125 us: local(): pl.pallas_call(kernel, out_shape=(jax.ShapeDtypeStruct((BELIEFS, W), f32)...]
    unnamed x2 -> x0, local copies, waits for them, and re-layouts: 2.92 us -> none
where the time goes in v2:
time: 128 us
  Pallas kernels  127 us (99%)
    pallas_call x1, Pallas kernels, local(): pl.pallas_call(kernel, out_shape=(jax.ShapeDtypeStruct((BELIEFS, W), f32)...  125 us

profile of v2, /device:TPU:1, one launch (start us, length us, event | category | flops | bytes accessed | tf_op | source)
XLA Modules:
  0.0 127.5 jit_solution(1576138796781507032)
XLA Ops:
  0.6 125.2 %chain.1 = (f32[512,128]{1,0:T(8,128)}, f32[16,4,128]{2,1,0:T(4,128)}) custom-call(s32[32,512]{1,0:T(8,128)} %bitcast.9, s32[1,512]{1,0:T(1,128)} %action_ref.1, f32[8,128]{1,0:T(8,128)} %reward_ref.1, f32[8,32,128]{2,1,0:T(8,128)} %obs_hbm.1, f32[512,128]{1,0:T(8,128)} %terminal_hbm.1, bf16[1024,2048]{1,0:T(8,128)(2,1)} %bitcast.7, f32[512,128]{1,0:T(8,128)} %bitcast.8), custom_call_target="tpu_custom_call" | custom-call | tf_op jit(solution)/shard_map/chain/pallas_call | solution.py:329
  125.9 1.7 %finish.1 = (f32[512,128]{1,0:T(8,128)}, f32[4,128]{1,0:T(4,128)}) custom-call(f32[512,128]{1,0:T(8,128)} %get-tuple-element.6.final_ref, f32[16,4,128]{2,1,0:T(4,128)} %get-tuple-element.7.vbuf_ref), custom_call_target="tpu_custom_call" | custom-call | tf_op jit(solution)/shard_map/finish/pallas_call | solution.py:379

commit v3 on v2

--- a/solution.py
+++ b/solution.py
@@ -26,10 +26,10 @@
 def kernel(
     next_ref, action_ref, reward_ref, obs_hbm, terminal_hbm, trans_hbm, belief_hbm,
     final, vbuf,
-    obs, trans, belief, nbuf, tab, idx, turned, onehot, weight, rewrow, masked,
-    pair_send, pair_recv, part_send, part_recv, sums_send, sums,
-    load_sem, idx_ssem, idx_rsem, pair_ssem, pair_rsem, part_ssem, part_rsem,
-    sums_ssem, sums_rsem, row_ssem, row_rsem, out_ssem, out_rsem, val_ssem, val_rsem,
+    obs, trans, belief, nbuf, tab, idx, turned, onehot, weight, reward, rewrow, masked,
+    pair_send, pair_recv, part_send, part_recv, fresh,
+    load_sem, idx_ssem, idx_rsem, reward_ssem, reward_rsem, pair_ssem, pair_rsem, part_ssem, part_rsem,
+    row_ssem, row_rsem, out_ssem, out_rsem, val_ssem, val_rsem,
 ):
     sec = lax.axis_index("section")
     st = lax.axis_index("state")
@@ -37,8 +37,10 @@
     core, chip = lax.rem(st, 2), lax.div(st, 2)
     lo, y = lax.div(chip, 4), lax.rem(chip, 4)
 
-    def rows_of(p):
-        return pl.ds(pl.multiple_of(p * BATCH, BATCH), BATCH)
+    mine = plane * 2 + half
+
+    def rows_of(m):
+        return pl.ds(pl.multiple_of(m * ROWS, ROWS), ROWS)
 
     def other_section(d):
         return lax.rem(sec + d, SECTIONS)
@@ -46,12 +48,12 @@
     def other_state(d):
         return lax.rem(st + d, SHARDS)
 
-    def other_plane(d):
-        return lax.rem(plane + d, PLANES)
-
-    def z_neighbour(up):
+    def z_neighbour(up, d):
         z = lax.rem(half * 2 + lo + (1 if up else 3), 4)
-        return {"section": lax.div(z, 2) * PLANES + plane, "state": (lax.rem(z, 2) * 4 + y) * 2 + core}
+        return {
+            "section": lax.div(z, 2) * PLANES + lax.rem(plane + d, PLANES),
+            "state": (lax.rem(z, 2) * 4 + y) * 2 + core,
+        }
 
     loads = [
         pltpu.make_async_copy(obs_hbm, obs, load_sem.at[0]),
@@ -68,7 +70,8 @@
     for d in range(1, SHARDS):
         pl.semaphore_signal(barrier, inc=1, device_id={"section": sec, "state": other_state(d)}, device_id_type=MESH)
     for up in (True, False):
-        pl.semaphore_signal(barrier, inc=1, device_id=z_neighbour(up), device_id_type=MESH)
+        for d in range(PLANES):
+            pl.semaphore_signal(barrier, inc=1, device_id=z_neighbour(up, d), device_id_type=MESH)
 
     for p in range(PLANES):
         tab[p, 0:OBS, :] = next_ref[:, p * BATCH : (p + 1) * BATCH]
@@ -80,7 +83,7 @@
                 nbuf[t, p * BATCH : (p + 1) * BATCH, :] = jnp.zeros((BATCH, W), jnp.float32)
     idx[pl.ds(sec, 1)] = tab[pl.ds(plane, 1)]
 
-    pl.semaphore_wait(barrier, SECTIONS + SHARDS)
+    pl.semaphore_wait(barrier, SECTIONS - 1 + SHARDS - 1 + 2 * PLANES)
 
     def idx_copy(d):
         to = other_section(d)
@@ -90,8 +93,16 @@
             device_id={"section": to, "state": st}, device_id_type=MESH,
         )
 
-    for d in range(1, SECTIONS):
-        idx_copy(d).start()
+    @pl.when(sec == SECTIONS - 1)
+    def _():
+        for d in range(1, SECTIONS):
+            idx_copy(d).start()
+
+    reward_copy = pltpu.make_async_remote_copy(
+        src_ref=reward_ref, dst_ref=reward, send_sem=reward_ssem, recv_sem=reward_rsem,
+        device_id=z_neighbour(True, 0), device_id_type=MESH,
+    )
+    reward_copy.start()
 
     def prepare(t):
         h = STEPS - 1 - t
@@ -104,13 +115,13 @@
             ).wait_recv()
 
         turned[...] = idx[h].T
-        act = turned[:, OBS : OBS + 1]
-        row = jnp.zeros((BATCH, W), jnp.float32)
+        table = turned[pl.ds(pl.multiple_of(half * ROWS, ROWS), ROWS), :]
+        act = table[:, OBS : OBS + 1]
+        row = jnp.zeros((ROWS, W), jnp.float32)
         for a in range(ACTIONS):
-            row = jnp.where(act == a, reward_ref[a : a + 1, :], row)
+            row = jnp.where(act == a, reward[a : a + 1, :], row)
         rewrow[lax.rem(t, 2)] = row
-        table = turned[pl.ds(pl.multiple_of(half * ROWS, ROWS), ROWS), :]
-        wide = jnp.broadcast_to(table[:, OBS : OBS + 1], (ROWS, W))
+        wide = jnp.broadcast_to(act, (ROWS, W))
         column = lax.broadcasted_iota(jnp.int32, (ROWS, BELIEFS), 1)
         for o in range(OBS):
             pick = table[:, o : o + 1]
@@ -141,60 +152,55 @@
             device_id={"section": sec, "state": chip_at(k, 0) * 2 + core}, device_id_type=MESH,
         )
 
-    def sums_copy(up, t):
-        return pltpu.make_async_remote_copy(
-            src_ref=sums_send, dst_ref=sums.at[t, half],
-            send_sem=sums_ssem.at[int(up)], recv_sem=sums_rsem.at[t, half],
-            device_id=z_neighbour(up), device_id_type=MESH,
-        )
-
-    def wait_sums(f, t):
+    users = tuple((d, up) for d in range(PLANES) for up in (True, False))
+
+    def row_copy(u, t):
+        d, up = users[u]
+        return pltpu.make_async_remote_copy(
+            src_ref=fresh.at[t], dst_ref=nbuf.at[t + 1, rows_of(mine)],
+            send_sem=row_ssem.at[u], recv_sem=row_rsem.at[t, mine],
+            device_id=z_neighbour(up, d), device_id_type=MESH,
+        )
+
+    def feeds(u, t):
+        return (plane + users[u][0] < PLANES) & (t < STEPS - 1)
+
+    def out_copy(t):
+        return pltpu.make_async_remote_copy(
+            src_ref=fresh.at[t], dst_ref=final.at[rows_of(mine)],
+            send_sem=out_ssem, recv_sem=out_rsem.at[mine],
+            device_id={"section": STEPS - 1 - t, "state": ((1 - lo) * 4 + y) * 2 + core},
+            device_id_type=MESH,
+        )
+
+    def goes_out(t):
+        return (lax.rem(STEPS - 1 - t, PLANES) < plane) | (t == STEPS - 1)
+
+    def wait_into(dst, sem):
         pltpu.make_async_remote_copy(
-            src_ref=sums_send, dst_ref=sums.at[t, f],
-            send_sem=sums_ssem.at[0], recv_sem=sums_rsem.at[t, f],
-            device_id=z_neighbour(True), device_id_type=MESH,
+            src_ref=fresh.at[0], dst_ref=dst, send_sem=out_ssem, recv_sem=sem,
+            device_id=z_neighbour(True, 0), device_id_type=MESH,
         ).wait_recv()
 
-    def row_copy(d, t):
-        return pltpu.make_async_remote_copy(
-            src_ref=nbuf.at[t + 1, rows_of(plane)], dst_ref=nbuf.at[t + 1, rows_of(plane)],
-            send_sem=row_ssem.at[d], recv_sem=row_rsem.at[t, plane],
-            device_id={"section": half * PLANES + other_plane(d), "state": st}, device_id_type=MESH,
-        )
-
-    def feeds(d, t):
-        return (other_plane(d) > plane) & (t < STEPS - 1)
-
-    def wait_rows(p, t):
-        pltpu.make_async_remote_copy(
-            src_ref=nbuf.at[t + 1, rows_of(p)], dst_ref=nbuf.at[t + 1, rows_of(p)],
-            send_sem=row_ssem.at[0], recv_sem=row_rsem.at[t, p],
-            device_id={"section": half * PLANES + other_plane(1), "state": st}, device_id_type=MESH,
-        ).wait_recv()
-
-    def out_copy(t):
-        return pltpu.make_async_remote_copy(
-            src_ref=nbuf.at[t + 1, rows_of(plane)], dst_ref=final.at[rows_of(plane)],
-            send_sem=out_ssem, recv_sem=out_rsem.at[plane],
-            device_id={"section": STEPS - 1 - t, "state": st}, device_id_type=MESH,
-        )
-
-    def goes_out(t):
-        owner = STEPS - 1 - t
-        return (lax.div(owner, PLANES) == half) & (lax.rem(owner, PLANES) < plane)
-
     def wait_sent(t):
-        for d in range(1, PLANES):
-            @pl.when(feeds(d, t))
+        for u in range(len(users)):
+            @pl.when(feeds(u, t))
             def _():
-                row_copy(d, t).wait_send()
+                row_copy(u, t).wait_send()
 
         @pl.when(goes_out(t))
         def _():
             out_copy(t).wait_send()
 
     loads[0].wait()
+    reward_copy.wait_recv()
     prepare(0)
+
+    @pl.when(sec < SECTIONS - 1)
+    def _():
+        for d in range(1, SECTIONS):
+            idx_copy(d).start()
+
     loads[1].wait()
     loads[2].wait()
 
@@ -243,54 +249,43 @@
         for k in range(CHIPS - 1):
             part_copy(k, t).wait_recv()
             summed = summed + part_recv[t, k]
-        sums_send[...] = summed
-        for up in (True, False):
-            sums_copy(up, t).start()
+        fresh[t] = rewrow[lax.rem(t, 2)] + discount * summed
+        for u in range(len(users)):
+            @pl.when(feeds(u, t))
+            def _():
+                row_copy(u, t).start()
+
+        @pl.when(goes_out(t))
+        def _():
+            out_copy(t).start()
+
         for k in range(CHIPS - 1):
             part_copy(k, t).wait_send()
-        for f in (0, 1):
-            wait_sums(f, t)
-        nbuf[t + 1, rows_of(plane)] = (
-            rewrow[lax.rem(t, 2)] + discount * sums[t].reshape(BATCH, W)
-        )
-        for d in range(1, PLANES):
-            @pl.when(feeds(d, t))
-            def _():
-                row_copy(d, t).start()
-
-        @pl.when(goes_out(t))
-        def _():
-            out_copy(t).start()
-
-        for up in (True, False):
-            sums_copy(up, t).wait_send()
 
         @pl.when(t < STEPS - 1)
         def _():
-            for p in range(PLANES - 1):
-                @pl.when(p < plane)
+            for m in range(2 * PLANES):
+                @pl.when(m // 2 <= plane)
                 def _():
-                    wait_rows(p, t)
+                    wait_into(nbuf.at[t + 1, rows_of(m)], row_rsem.at[t, m])
 
         return carry
 
     lax.fori_loop(0, STEPS, step, 0)
 
     own = STEPS - 1 - sec
-    for p in range(PLANES):
-        @pl.when(p <= plane)
-        def _():
-            final[p * BATCH : (p + 1) * BATCH, :] = nbuf[own + 1, p * BATCH : (p + 1) * BATCH, :]
-
     loads[3].wait()
     for p in range(PLANES):
-        @pl.when(p > plane)
-        def _():
-            pltpu.make_async_remote_copy(
-                src_ref=final.at[rows_of(p)], dst_ref=final.at[rows_of(p)],
-                send_sem=out_ssem, recv_sem=out_rsem.at[p],
-                device_id={"section": half * PLANES + other_plane(1), "state": st}, device_id_type=MESH,
-            ).wait_recv()
+        used = (p <= plane) & (sec > 0)
+
+        @pl.when(used)
+        def _():
+            final[p * BATCH : (p + 1) * BATCH, :] = nbuf[own + 1, p * BATCH : (p + 1) * BATCH, :]
+
+        @pl.when(jnp.logical_not(used))
+        def _():
+            for m in (2 * p, 2 * p + 1):
+                wait_into(final.at[rows_of(m)], out_rsem.at[m])
 
         block = final[p * BATCH : (p + 1) * BATCH, :] * belief[p * BATCH : (p + 1) * BATCH, :]
         vbuf[pl.ds(st, 1), p : p + 1, :] = jnp.sum(block.T, axis=0, keepdims=True)[None]
@@ -305,6 +300,7 @@
     for d in range(1, SHARDS):
         val_copy(d).start()
     wait_sent(STEPS - 1)
+    reward_copy.wait_send()
     for d in range(1, SECTIONS):
         idx_copy(d).wait_send()
     for d in range(1, SHARDS):
@@ -344,27 +340,27 @@
             pltpu.VMEM((BATCH, TAB), jnp.int32),
             pltpu.VMEM((OBS * ROWS, BELIEFS), jnp.bfloat16),
             pltpu.VMEM((OBS, ROWS, W), f32),
-            pltpu.VMEM((2, BATCH, W), f32),
+            pltpu.VMEM((ACTIONS, W), f32),
+            pltpu.VMEM((2, ROWS, W), f32),
             pltpu.VMEM((ROWS, ACTIONS * W), jnp.bfloat16),
             pltpu.VMEM((CHIPS, ROWS, W), f32),
             pltpu.VMEM((STEPS, CHIPS, ROWS, W), f32),
             pltpu.VMEM((CHIPS, ROWS, W), f32),
             pltpu.VMEM((STEPS, CHIPS, ROWS, W), f32),
-            pltpu.VMEM((ROWS, W), f32),
-            pltpu.VMEM((STEPS, 2, ROWS, W), f32),
+            pltpu.VMEM((STEPS, ROWS, W), f32),
             dma((4,)),
             dma((SECTIONS,)),
             dma((SECTIONS,)),
+            dma,
+            dma,
             dma((CHIPS,)),
             dma((STEPS, CHIPS)),
             dma((CHIPS,)),
             dma((STEPS, CHIPS)),
-            dma((2,)),
-            dma((STEPS, 2)),
-            dma((PLANES,)),
-            dma((STEPS, PLANES)),
+            dma((2 * PLANES,)),
+            dma((STEPS, 2 * PLANES)),
             dma,
-            dma((PLANES,)),
+            dma((2 * PLANES,)),
             dma((SHARDS,)),
             dma((SHARDS,)),
         ],

time: 128 us -> 125 us (0.977)
  Pallas kernels: 127 us -> 124 us
    pallas_call x1, Pallas kernels: 125 us -> 123 us  [local(): pl.pallas_call(kernel, out_shape=(jax.ShapeDtypeStruct((BELIEFS, W), f32)...]
where the time goes in v3:
time: 125 us
  Pallas kernels  124 us (99%)
    pallas_call x1, Pallas kernels, local(): pl.pallas_call(kernel, out_shape=(jax.ShapeDtypeStruct((BELIEFS, W), f32)...  123 us

profile of v3, /device:TPU:1, one launch (start us, length us, event | category | flops | bytes accessed | tf_op | source)
XLA Modules:
  0.0 124.9 jit_solution(8865782427654799094)
XLA Ops:
  0.6 122.6 %chain.1 = (f32[512,128]{1,0:T(8,128)}, f32[16,4,128]{2,1,0:T(4,128)}) custom-call(s32[32,512]{1,0:T(8,128)} %bitcast.9, s32[1,512]{1,0:T(1,128)} %action_ref.1, f32[8,128]{1,0:T(8,128)} %reward_ref.1, f32[8,32,128]{2,1,0:T(8,128)} %obs_hbm.1, f32[512,128]{1,0:T(8,128)} %terminal_hbm.1, bf16[1024,2048]{1,0:T(8,128)(2,1)} %bitcast.7, f32[512,128]{1,0:T(8,128)} %bitcast.8), custom_call_target="tpu_custom_call" | custom-call | tf_op jit(solution)/shard_map/chain/pallas_call | solution.py:325
  123.2 1.7 %finish.1 = (f32[512,128]{1,0:T(8,128)}, f32[4,128]{1,0:T(4,128)}) custom-call(f32[512,128]{1,0:T(8,128)} %get-tuple-element.6.final_ref, f32[16,4,128]{2,1,0:T(4,128)} %get-tuple-element.7.vbuf_ref), custom_call_target="tpu_custom_call" | custom-call | tf_op jit(solution)/shard_map/finish/pallas_call | solution.py:375

commit v4 on v3

v4 whole, which is shorter than its diff:
```python
import jax
import jax.numpy as jnp
from jax import lax
from jax.experimental import pallas as pl
from jax.experimental.pallas import tpu as pltpu
from jax.sharding import PartitionSpec as P

MESH = pl.DeviceIdType.MESH
discount = 0.95

ACTIONS = 8
OBS = 32
STEPS = 8
SECTIONS = 8
PLANES = 4
CHIPS = 8
SHARDS = 16
BELIEFS = 512
BATCH = 128
ROWS = 64
W = 128
FOLD = 256
TAB = 40
GROUP = 8


def kernel(
    next_ref, action_ref, reward_ref, obs_hbm, terminal_hbm, trans_hbm, belief_hbm,
    final, vbuf,
    obs, trans, belief, nbuf, tab, idx, turned, onehot, weight, rewrow, masked,
    pair_send, pair_recv, part_send, part_recv,
    load_sem, idx_ssem, idx_rsem, pair_ssem, pair_rsem, part_ssem, part_rsem,
    row_ssem, row_rsem, out_ssem, out_rsem, val_ssem, val_rsem,
):
    sec = lax.axis_index("section")
    st = lax.axis_index("state")
    plane, half = lax.rem(sec, PLANES), lax.div(sec, PLANES)
    core, chip = lax.rem(st, 2), lax.div(st, 2)
    lo, y = lax.div(chip, 4), lax.rem(chip, 4)

    def rows_of(p, q):
        return pl.ds(pl.multiple_of((p * 2 + q) * ROWS, ROWS), ROWS)

    def other_section(d):
        return lax.rem(sec + d, SECTIONS)

    def other_state(d):
        return lax.rem(st + d, SHARDS)

    def other_plane(d):
        return lax.rem(plane + d, PLANES)

    def z_neighbour(up, dy):
        z = lax.rem(half * 2 + lo + (1 if up else 3), 4)
        return {
            "section": lax.div(z, 2) * PLANES + plane,
            "state": (lax.rem(z, 2) * 4 + lax.rem(y + dy, 4)) * 2 + core,
        }

    loads = [
        pltpu.make_async_copy(obs_hbm, obs, load_sem.at[0]),
        pltpu.make_async_copy(terminal_hbm, nbuf.at[0], load_sem.at[1]),
        pltpu.make_async_copy(trans_hbm, trans, load_sem.at[2]),
        pltpu.make_async_copy(belief_hbm, belief, load_sem.at[3]),
    ]
    for load in loads:
        load.start()

    barrier = pltpu.get_barrier_semaphore()
    for d in range(1, SECTIONS):
        pl.semaphore_signal(barrier, inc=1, device_id={"section": other_section(d), "state": st}, device_id_type=MESH)
    for d in range(1, SHARDS):
        pl.semaphore_signal(barrier, inc=1, device_id={"section": sec, "state": other_state(d)}, device_id_type=MESH)
    for up in (True, False):
        for dy in range(4):
            pl.semaphore_signal(barrier, inc=1, device_id=z_neighbour(up, dy), device_id_type=MESH)

    for p in range(PLANES):
        tab[p, 0:OBS, :] = next_ref[:, p * BATCH : (p + 1) * BATCH]
        tab[p, OBS : OBS + 1, :] = action_ref[:, p * BATCH : (p + 1) * BATCH]
        tab[p, OBS + 1 :, :] = jnp.zeros((TAB - OBS - 1, BATCH), jnp.int32)
        for t in range(1, STEPS):
            @pl.when(p > plane)
            def _():
                nbuf[t, p * BATCH : (p + 1) * BATCH, :] = jnp.zeros((BATCH, W), jnp.float32)
    idx[pl.ds(sec, 1)] = tab[pl.ds(plane, 1)]

    pl.semaphore_wait(barrier, SECTIONS - 1 + SHARDS - 1 + 8)

    def idx_copy(d):
        to = other_section(d)
        return pltpu.make_async_remote_copy(
            src_ref=tab.at[lax.rem(to, PLANES)], dst_ref=idx.at[sec],
            send_sem=idx_ssem.at[d], recv_sem=idx_rsem.at[sec],
            device_id={"section": to, "state": st}, device_id_type=MESH,
        )

    @pl.when(sec == SECTIONS - 1)
    def _():
        for d in range(1, SECTIONS):
            idx_copy(d).start()

    def prepare(t):
        h = STEPS - 1 - t

        @pl.when(h != sec)
        def _():
            pltpu.make_async_remote_copy(
                src_ref=idx.at[h], dst_ref=idx.at[h], send_sem=idx_ssem.at[0], recv_sem=idx_rsem.at[h],
                device_id={"section": sec, "state": other_state(1)}, device_id_type=MESH,
            ).wait_recv()

        turned[...] = idx[h].T
        act = turned[:, OBS : OBS + 1]
        row = jnp.zeros((BATCH, W), jnp.float32)
        for a in range(ACTIONS):
            row = jnp.where(act == a, reward_ref[a : a + 1, :], row)
        rewrow[lax.rem(t, 2)] = row
        wide = jnp.broadcast_to(act, (BATCH, W))
        column = lax.broadcasted_iota(jnp.int32, (BATCH, FOLD), 1)
        for o in range(OBS):
            pick = turned[:, o : o + 1]
            hit = jnp.where(column == lax.rem(pick, FOLD), 1.0, 0.0).astype(jnp.bfloat16)
            w = jnp.zeros((BATCH, W), jnp.float32)
            for a in range(ACTIONS):
                w = jnp.where(wide == a, obs[a, o : o + 1, :], w)
            upper = jnp.broadcast_to(pick >= FOLD, (BATCH, W))
            w_low, w_up = jnp.where(upper, 0.0, w), jnp.where(upper, w, 0.0)
            for q in (0, 1):
                onehot[q, o * ROWS : (o + 1) * ROWS, :] = hit[q * ROWS : (q + 1) * ROWS, :]
                weight[q, o, :, :W] = w_low[q * ROWS : (q + 1) * ROWS, :]
                weight[q, o, :, W:] = w_up[q * ROWS : (q + 1) * ROWS, :]

    order = ((1, 2), (0, 2), (1, 1), (1, 3), (0, 1), (0, 3), (1, 0), (0, 0))

    def block_at(k):
        return lax.rem(lo + order[k][0], 2) * 4 + lax.rem(y + order[k][1], 4)

    def user_of(q, k):
        if order[k][0]:
            return z_neighbour(q == 0, order[k][1])
        return {"section": sec, "state": block_at(k) * 2 + core}

    def pair_copy(q, k, t):
        return pltpu.make_async_remote_copy(
            src_ref=pair_send.at[q, k], dst_ref=pair_recv.at[t, q, k],
            send_sem=pair_ssem.at[q, k], recv_sem=pair_rsem.at[t, q, k],
            device_id={"section": sec, "state": chip * 2 + 1 - core}, device_id_type=MESH,
        )

    def part_copy(q, k, t):
        return pltpu.make_async_remote_copy(
            src_ref=part_send.at[q, k], dst_ref=part_recv.at[t, q, k],
            send_sem=part_ssem.at[q, k], recv_sem=part_rsem.at[t, q, k],
            device_id=user_of(q, k), device_id_type=MESH,
        )

    def row_copy(q, d, t):
        return pltpu.make_async_remote_copy(
            src_ref=nbuf.at[t + 1, rows_of(plane, q)], dst_ref=nbuf.at[t + 1, rows_of(plane, q)],
            send_sem=row_ssem.at[q, d], recv_sem=row_rsem.at[t, plane, q],
            device_id={"section": half * PLANES + other_plane(d), "state": st}, device_id_type=MESH,
        )

    def feeds(d, t):
        return (plane + d < PLANES) & (t < STEPS - 1)

    def out_copy(q, t):
        return pltpu.make_async_remote_copy(
            src_ref=nbuf.at[t + 1, rows_of(plane, q)], dst_ref=final.at[rows_of(plane, q)],
            send_sem=out_ssem.at[q], recv_sem=out_rsem.at[plane, q],
            device_id={"section": STEPS - 1 - t, "state": st}, device_id_type=MESH,
        )

    def goes_out(t):
        owner = STEPS - 1 - t
        return (lax.div(owner, PLANES) == half) & (lax.rem(owner, PLANES) < plane)

    def wait_into(dst, sem):
        pltpu.make_async_remote_copy(
            src_ref=pair_send.at[0, 0], dst_ref=dst, send_sem=out_ssem.at[0], recv_sem=sem,
            device_id={"section": half * PLANES + other_plane(1), "state": st}, device_id_type=MESH,
        ).wait_recv()

    def wait_sent(t):
        for q in (0, 1):
            for d in range(1, PLANES):
                @pl.when(feeds(d, t))
                def _():
                    row_copy(q, d, t).wait_send()

            @pl.when(goes_out(t))
            def _():
                out_copy(q, t).wait_send()

    loads[0].wait()
    prepare(0)

    @pl.when(sec < SECTIONS - 1)
    def _():
        for d in range(1, SECTIONS):
            idx_copy(d).start()

    loads[1].wait()
    loads[2].wait()

    def gather(q, folded):
        total = jnp.zeros((ROWS, 2 * W), jnp.float32)
        for c in range(OBS // GROUP):
            got = jnp.dot(
                onehot[q, c * GROUP * ROWS : (c + 1) * GROUP * ROWS, :], folded,
                preferred_element_type=jnp.float32,
            ).reshape(GROUP, ROWS, 2 * W)
            total = total + jnp.sum(got * weight[q, c * GROUP : (c + 1) * GROUP], axis=0)
        total = total[:, :W] + total[:, W:]
        act = turned[q * ROWS : (q + 1) * ROWS, OBS : OBS + 1]
        for a in range(ACTIONS):
            masked[q, :, a * W : (a + 1) * W] = jnp.where(act == a, total, 0.0).astype(jnp.bfloat16)

    def multiply(q, t):
        for k in range(CHIPS):
            part = jnp.dot(
                masked[q], trans[:, pl.ds(pl.multiple_of(block_at(k) * 2 * W, 2 * W), 2 * W)],
                preferred_element_type=jnp.float32,
            )
            pair_send[q, k] = jnp.where(core == 0, part[:, W:], part[:, :W])
            pair_copy(q, k, t).start()
            part_send[q, k] = jnp.where(core == 0, part[:, :W], part[:, W:])

    def send_parts(q, t):
        for k in range(CHIPS):
            pair_copy(q, k, t).wait_recv()
            part_send[q, k] = part_send[q, k] + pair_recv[t, q, k]
            if k < CHIPS - 1:
                part_copy(q, k, t).start()

    def add_parts(q, t):
        summed = part_send[q, CHIPS - 1]
        for k in range(CHIPS - 1):
            part_copy(q, k, t).wait_recv()
            summed = summed + part_recv[t, q, k]
        nbuf[t + 1, rows_of(plane, q)] = (
            rewrow[lax.rem(t, 2), q * ROWS : (q + 1) * ROWS, :] + discount * summed
        )
        for d in range(1, PLANES):
            @pl.when(feeds(d, t))
            def _():
                row_copy(q, d, t).start()

        @pl.when(goes_out(t))
        def _():
            out_copy(q, t).start()

    def step(t, carry):
        following = nbuf[t].astype(jnp.bfloat16)
        folded = jnp.concatenate([following[:FOLD], following[FOLD:]], axis=1)
        gather(0, folded)
        multiply(0, t)
        gather(1, folded)
        send_parts(0, t)
        multiply(1, t)
        send_parts(1, t)

        @pl.when(t > 0)
        def _():
            wait_sent(t - 1)

        @pl.when(t < STEPS - 1)
        def _():
            prepare(t + 1)

        for q in (0, 1):
            for k in range(CHIPS):
                pair_copy(q, k, t).wait_send()
        for q in (0, 1):
            add_parts(q, t)
            for k in range(CHIPS - 1):
                part_copy(q, k, t).wait_send()

        @pl.when(t < STEPS - 1)
        def _():
            for p in range(PLANES - 1):
                @pl.when(p < plane)
                def _():
                    for q in (0, 1):
                        wait_into(nbuf.at[t + 1, rows_of(p, q)], row_rsem.at[t, p, q])

        return carry

    lax.fori_loop(0, STEPS, step, 0)

    own = STEPS - 1 - sec
    for p in range(PLANES):
        @pl.when(p <= plane)
        def _():
            final[p * BATCH : (p + 1) * BATCH, :] = nbuf[own + 1, p * BATCH : (p + 1) * BATCH, :]

    loads[3].wait()
    for p in range(PLANES):
        @pl.when(p > plane)
        def _():
            for q in (0, 1):
                wait_into(final.at[rows_of(p, q)], out_rsem.at[p, q])

        block = final[p * BATCH : (p + 1) * BATCH, :] * belief[p * BATCH : (p + 1) * BATCH, :]
        vbuf[pl.ds(st, 1), p : p + 1, :] = jnp.sum(block.T, axis=0, keepdims=True)[None]

    def val_copy(d):
        return pltpu.make_async_remote_copy(
            src_ref=vbuf.at[st], dst_ref=vbuf.at[st],
            send_sem=val_ssem.at[d], recv_sem=val_rsem.at[d],
            device_id={"section": sec, "state": other_state(d)}, device_id_type=MESH,
        )

    for d in range(1, SHARDS):
        val_copy(d).start()
    wait_sent(STEPS - 1)
    for d in range(1, SECTIONS):
        idx_copy(d).wait_send()
    for d in range(1, SHARDS):
        val_copy(d).wait_recv()
    for d in range(1, SHARDS):
        val_copy(d).wait_send()


def finish(final_ref, vbuf_ref, alphas_ref, values_ref):
    alphas_ref[...] = final_ref[...]
    value = vbuf_ref[0]
    for s in range(1, SHARDS):
        value = value + vbuf_ref[s]
    values_ref[...] = value


def local(belief, action, next_index, obs_table, transition, reward, terminal):
    vmem = pl.BlockSpec(memory_space=pltpu.VMEM)
    anywhere = pl.BlockSpec(memory_space=pl.ANY)
    dma = pltpu.SemaphoreType.DMA
    f32 = jnp.float32
    final, parts = pl.pallas_call(
        kernel,
        out_shape=(
            jax.ShapeDtypeStruct((BELIEFS, W), f32),
            jax.ShapeDtypeStruct((SHARDS, PLANES, W), f32),
        ),
        in_specs=[vmem, vmem, vmem, anywhere, anywhere, anywhere, anywhere],
        out_specs=(vmem, vmem),
        scratch_shapes=[
            pltpu.VMEM((ACTIONS, OBS, W), f32),
            pltpu.VMEM((ACTIONS * W, SHARDS * W), jnp.bfloat16),
            pltpu.VMEM((BELIEFS, W), f32),
            pltpu.VMEM((STEPS + 1, BELIEFS, W), f32),
            pltpu.VMEM((PLANES, TAB, BATCH), jnp.int32),
            pltpu.VMEM((SECTIONS, TAB, BATCH), jnp.int32),
            pltpu.VMEM((BATCH, TAB), jnp.int32),
            pltpu.VMEM((2, OBS * ROWS, FOLD), jnp.bfloat16),
            pltpu.VMEM((2, OBS, ROWS, 2 * W), f32),
            pltpu.VMEM((2, BATCH, W), f32),
            pltpu.VMEM((2, ROWS, ACTIONS * W), jnp.bfloat16),
            pltpu.VMEM((2, CHIPS, ROWS, W), f32),
            pltpu.VMEM((STEPS, 2, CHIPS, ROWS, W), f32),
            pltpu.VMEM((2, CHIPS, ROWS, W), f32),
            pltpu.VMEM((STEPS, 2, CHIPS, ROWS, W), f32),
            dma((4,)),
            dma((SECTIONS,)),
            dma((SECTIONS,)),
            dma((2, CHIPS)),
            dma((STEPS, 2, CHIPS)),
            dma((2, CHIPS)),
            dma((STEPS, 2, CHIPS)),
            dma((2, PLANES)),
            dma((STEPS, PLANES, 2)),
            dma((2,)),
            dma((PLANES, 2)),
            dma((SHARDS,)),
            dma((SHARDS,)),
        ],
        compiler_params=pltpu.CompilerParams(
            collective_id=0, has_side_effects=True, vmem_limit_bytes=60 * 1024 * 1024
        ),
        name="chain",
    )(
        next_index[0].T, action, reward, obs_table, terminal,
        transition.reshape(ACTIONS * W, SHARDS * W), belief[0],
    )
    alphas, values = pl.pallas_call(
        finish,
        out_shape=(
            jax.ShapeDtypeStruct((BELIEFS, W), f32),
            jax.ShapeDtypeStruct((PLANES, W), f32),
        ),
        in_specs=[vmem, vmem],
        out_specs=(vmem, vmem),
        name="finish",
    )(final, parts)
    return alphas[None], values.reshape(1, BELIEFS)


def solution(mesh):
    return jax.shard_map(
        local,
        mesh=mesh,
        in_specs=(
            P("section", None, "state"),
            P("section", None),
            P("section", None, None),
            P(None, None, "state"),
            P(None, "state", None),
            P(None, "state"),
            P(None, "state"),
        ),
        out_specs=(P("section", None, "state"), P("section", None)),
        check_vma=False,
    )
```

time: 125 us -> 131 us (1.048)
  Pallas kernels: 124 us -> 130 us
    pallas_call x1, Pallas kernels: 123 us -> 129 us  [local(): pl.pallas_call(kernel, out_shape=(jax.ShapeDtypeStruct((BELIEFS, W), f32)...]
where the time goes in v4:
time: 131 us
  Pallas kernels  130 us (99%)
    pallas_call x1, Pallas kernels, local(): pl.pallas_call(kernel, out_shape=(jax.ShapeDtypeStruct((BELIEFS, W), f32)...  129 us

profile of v4, /device:TPU:1, one launch (start us, length us, event | category | flops | bytes accessed | tf_op | source)
XLA Modules:
  0.0 130.9 jit_solution(14947126660475398127)
XLA Ops:
  0.6 128.6 %chain.1 = (f32[512,128]{1,0:T(8,128)}, f32[16,4,128]{2,1,0:T(4,128)}) custom-call(s32[32,512]{1,0:T(8,128)} %bitcast.9, s32[1,512]{1,0:T(1,128)} %action_ref.1, f32[8,128]{1,0:T(8,128)} %reward_ref.1, f32[8,32,128]{2,1,0:T(8,128)} %obs_hbm.1, f32[512,128]{1,0:T(8,128)} %terminal_hbm.1, bf16[1024,2048]{1,0:T(8,128)(2,1)} %bitcast.7, f32[512,128]{1,0:T(8,128)} %bitcast.8), custom_call_target="tpu_custom_call" | custom-call | tf_op jit(solution)/shard_map/chain/pallas_call | solution.py:339
  129.2 1.7 %finish.1 = (f32[512,128]{1,0:T(8,128)}, f32[4,128]{1,0:T(4,128)}) custom-call(f32[512,128]{1,0:T(8,128)} %get-tuple-element.6.final_ref, f32[16,4,128]{2,1,0:T(4,128)} %get-tuple-element.7.vbuf_ref), custom_call_target="tpu_custom_call" | custom-call | tf_op jit(solution)/shard_map/finish/pallas_call | solution.py:385

commit v5 on v3

--- a/solution.py
+++ b/solution.py
@@ -19,8 +19,11 @@
 BATCH = 128
 ROWS = 64
 W = 128
+FOLD = 256
 TAB = 40
 GROUP = 8
+GROUPS = ((0,), (1, 2), (3, 4), (5, 6, 7))
+LAST = STEPS - 1
 
 
 def kernel(
@@ -28,7 +31,7 @@
     final, vbuf,
     obs, trans, belief, nbuf, tab, idx, turned, onehot, weight, reward, rewrow, masked,
     pair_send, pair_recv, part_send, part_recv, fresh,
-    load_sem, idx_ssem, idx_rsem, reward_ssem, reward_rsem, pair_ssem, pair_rsem, part_ssem, part_rsem,
+    bel, vsend, own_ssem, own_rsem, load_sem, bel_ssem, bel_rsem, idx_ssem, idx_rsem, reward_ssem, reward_rsem, pair_ssem, pair_rsem, part_ssem, part_rsem,
     row_ssem, row_rsem, out_ssem, out_rsem, val_ssem, val_rsem,
 ):
     sec = lax.axis_index("section")
@@ -95,7 +98,7 @@
 
     @pl.when(sec == SECTIONS - 1)
     def _():
-        for d in range(1, SECTIONS):
+        for d in (1, 5, 2, 6, 3, 7, 4):
             idx_copy(d).start()
 
     reward_copy = pltpu.make_async_remote_copy(
@@ -122,16 +125,18 @@
             row = jnp.where(act == a, reward[a : a + 1, :], row)
         rewrow[lax.rem(t, 2)] = row
         wide = jnp.broadcast_to(act, (ROWS, W))
-        column = lax.broadcasted_iota(jnp.int32, (ROWS, BELIEFS), 1)
+        column = lax.broadcasted_iota(jnp.int32, (ROWS, FOLD), 1)
         for o in range(OBS):
             pick = table[:, o : o + 1]
             onehot[o * ROWS : (o + 1) * ROWS, :] = (
-                jnp.where(column == pick, 1.0, 0.0).astype(jnp.bfloat16)
+                jnp.where(column == lax.rem(pick, FOLD), 1.0, 0.0).astype(jnp.bfloat16)
             )
             w = jnp.zeros((ROWS, W), jnp.float32)
             for a in range(ACTIONS):
                 w = jnp.where(wide == a, obs[a, o : o + 1, :], w)
-            weight[o] = w
+            upper = jnp.broadcast_to(pick >= FOLD, (ROWS, W))
+            weight[o, :, :W] = jnp.where(upper, 0.0, w)
+            weight[o, :, W:] = jnp.where(upper, w, 0.0)
 
     order = ((1, 2), (0, 2), (1, 1), (1, 3), (0, 1), (0, 3), (1, 0), (0, 0))
 
@@ -175,6 +180,23 @@
 
     def goes_out(t):
         return (lax.rem(STEPS - 1 - t, PLANES) < plane) | (t == STEPS - 1)
+
+    def bel_copy(m):
+        return pltpu.make_async_remote_copy(
+            src_ref=belief.at[m * ROWS : (m + 1) * ROWS], dst_ref=bel,
+            send_sem=bel_ssem.at[m], recv_sem=bel_rsem,
+            device_id={"section": (m % 2) * PLANES + m // 2, "state": ((1 - lo) * 4 + y) * 2 + core},
+            device_id_type=MESH,
+        )
+
+    def own_val_copy(s):
+        return pltpu.make_async_remote_copy(
+            src_ref=vsend, dst_ref=vbuf.at[st, pl.ds(mine, 1)], send_sem=own_ssem.at[s], recv_sem=own_rsem.at[mine],
+            device_id={"section": 0, "state": s}, device_id_type=MESH,
+        )
+
+    def elsewhere(s):
+        return (sec > 0) | (st != s)
 
     def wait_into(dst, sem):
         pltpu.make_async_remote_copy(
@@ -205,30 +227,33 @@
     loads[2].wait()
 
     def step(t, carry):
-        following = nbuf[t]
-        high = following.astype(jnp.bfloat16)
-        low = (following - high.astype(jnp.float32)).astype(jnp.bfloat16)
-        both = jnp.concatenate([high, low], axis=1)
-        total = jnp.zeros((ROWS, W), jnp.float32)
+        following = nbuf[t].astype(jnp.bfloat16)
+        folded = jnp.concatenate([following[:FOLD], following[FOLD:]], axis=1)
+        total = jnp.zeros((ROWS, 2 * W), jnp.float32)
         for c in range(OBS // GROUP):
             got = jnp.dot(
-                onehot[c * GROUP * ROWS : (c + 1) * GROUP * ROWS, :], both,
+                onehot[c * GROUP * ROWS : (c + 1) * GROUP * ROWS, :], folded,
                 preferred_element_type=jnp.float32,
-            )
-            got = (got[:, :W] + got[:, W:]).reshape(GROUP, ROWS, W)
+            ).reshape(GROUP, ROWS, 2 * W)
             total = total + jnp.sum(got * weight[c * GROUP : (c + 1) * GROUP], axis=0)
+        total = total[:, :W] + total[:, W:]
         act = turned[pl.ds(pl.multiple_of(half * ROWS, ROWS), ROWS), :][:, OBS : OBS + 1]
         for a in range(ACTIONS):
             masked[:, a * W : (a + 1) * W] = jnp.where(act == a, total, 0.0).astype(jnp.bfloat16)
 
-        for k in range(CHIPS):
-            part = jnp.dot(
-                masked[...], trans[:, pl.ds(pl.multiple_of(chip_at(k, 1) * 2 * W, 2 * W), 2 * W)],
-                preferred_element_type=jnp.float32,
-            )
-            pair_send[k] = jnp.where(core == 0, part[:, W:], part[:, :W])
-            pair_copy(k, t).start()
-            part_send[k] = jnp.where(core == 0, part[:, :W], part[:, W:])
+        for group in GROUPS:
+            parts = [
+                jnp.dot(
+                    masked[...], trans[:, pl.ds(pl.multiple_of(chip_at(k, 1) * 2 * W, 2 * W), 2 * W)],
+                    preferred_element_type=jnp.float32,
+                )
+                for k in group
+            ]
+            for k, part in zip(group, parts):
+                pair_send[k] = jnp.where(core == 0, part[:, W:], part[:, :W])
+                part_send[k] = jnp.where(core == 0, part[:, :W], part[:, W:])
+            for k in group:
+                pair_copy(k, t).start()
         for k in range(CHIPS):
             pair_copy(k, t).wait_recv()
             part_send[k] = part_send[k] + pair_recv[t, k]
@@ -259,6 +284,26 @@
         def _():
             out_copy(t).start()
 
+        @pl.when((t == LAST - 2) & (sec == 0))
+        def _():
+            loads[3].wait()
+            for m in range(2 * PLANES):
+                bel_copy(m).start()
+
+        @pl.when(t == LAST)
+        def _():
+            bel_copy(0).wait_recv()
+            product = fresh[t] * bel[...]
+            nothing = jnp.zeros((ROWS, W), jnp.float32)
+            first = jnp.concatenate([product, nothing], axis=0)
+            second = jnp.concatenate([nothing, product], axis=0)
+            both = jnp.where(half == 0, first, second)
+            vsend[...] = jnp.sum(both.T, axis=0, keepdims=True)
+            for s in range(SHARDS):
+                @pl.when(elsewhere(s))
+                def _():
+                    own_val_copy(s).start()
+
         for k in range(CHIPS - 1):
             part_copy(k, t).wait_send()
 
@@ -274,7 +319,11 @@
     lax.fori_loop(0, STEPS, step, 0)
 
     own = STEPS - 1 - sec
-    loads[3].wait()
+
+    @pl.when(sec > 0)
+    def _():
+        loads[3].wait()
+
     for p in range(PLANES):
         used = (p <= plane) & (sec > 0)
 
@@ -286,9 +335,6 @@
         def _():
             for m in (2 * p, 2 * p + 1):
                 wait_into(final.at[rows_of(m)], out_rsem.at[m])
-
-        block = final[p * BATCH : (p + 1) * BATCH, :] * belief[p * BATCH : (p + 1) * BATCH, :]
-        vbuf[pl.ds(st, 1), p : p + 1, :] = jnp.sum(block.T, axis=0, keepdims=True)[None]
 
     def val_copy(d):
         return pltpu.make_async_remote_copy(
@@ -297,16 +343,46 @@
             device_id={"section": sec, "state": other_state(d)}, device_id_type=MESH,
         )
 
-    for d in range(1, SHARDS):
-        val_copy(d).start()
+    @pl.when(sec > 0)
+    def _():
+        for p in range(PLANES):
+            block = final[p * BATCH : (p + 1) * BATCH, :] * belief[p * BATCH : (p + 1) * BATCH, :]
+            vbuf[pl.ds(st, 1), 2 * p : 2 * p + 1, :] = jnp.sum(block.T, axis=0, keepdims=True)[None]
+            vbuf[pl.ds(st, 1), 2 * p + 1 : 2 * p + 2, :] = jnp.zeros((1, 1, W), jnp.float32)
+        for d in range(1, SHARDS):
+            val_copy(d).start()
+
+    @pl.when(sec == 0)
+    def _():
+        vbuf[pl.ds(st, 1), 0:1, :] = vsend[...][None]
+        for m in range(2 * PLANES):
+            count = SHARDS if m else SHARDS - 1
+            pltpu.make_async_remote_copy(
+                src_ref=vbuf.at[pl.ds(0, count), m], dst_ref=vbuf.at[pl.ds(0, count), m],
+                send_sem=own_ssem.at[0], recv_sem=own_rsem.at[m],
+                device_id=z_neighbour(True, 0), device_id_type=MESH,
+            ).wait_recv()
+
     wait_sent(STEPS - 1)
     reward_copy.wait_send()
     for d in range(1, SECTIONS):
         idx_copy(d).wait_send()
-    for d in range(1, SHARDS):
-        val_copy(d).wait_recv()
-    for d in range(1, SHARDS):
-        val_copy(d).wait_send()
+    for s in range(SHARDS):
+        @pl.when(elsewhere(s))
+        def _():
+            own_val_copy(s).wait_send()
+
+    @pl.when(sec == 0)
+    def _():
+        for m in range(2 * PLANES):
+            bel_copy(m).wait_send()
+
+    @pl.when(sec > 0)
+    def _():
+        for d in range(1, SHARDS):
+            val_copy(d).wait_recv()
+        for d in range(1, SHARDS):
+            val_copy(d).wait_send()
 
 
 def finish(final_ref, vbuf_ref, alphas_ref, values_ref):
@@ -314,7 +390,8 @@
     value = vbuf_ref[0]
     for s in range(1, SHARDS):
         value = value + vbuf_ref[s]
-    values_ref[...] = value
+    for p in range(PLANES):
+        values_ref[p : p + 1, :] = value[2 * p : 2 * p + 1, :] + value[2 * p + 1 : 2 * p + 2, :]
 
 
 def local(belief, action, next_index, obs_table, transition, reward, terminal):
@@ -326,7 +403,7 @@
         kernel,
         out_shape=(
             jax.ShapeDtypeStruct((BELIEFS, W), f32),
-            jax.ShapeDtypeStruct((SHARDS, PLANES, W), f32),
+            jax.ShapeDtypeStruct((SHARDS, 2 * PLANES, W), f32),
         ),
         in_specs=[vmem, vmem, vmem, anywhere, anywhere, anywhere, anywhere],
         out_specs=(vmem, vmem),
@@ -338,8 +415,8 @@
             pltpu.VMEM((PLANES, TAB, BATCH), jnp.int32),
             pltpu.VMEM((SECTIONS, TAB, BATCH), jnp.int32),
             pltpu.VMEM((BATCH, TAB), jnp.int32),
-            pltpu.VMEM((OBS * ROWS, BELIEFS), jnp.bfloat16),
-            pltpu.VMEM((OBS, ROWS, W), f32),
+            pltpu.VMEM((OBS * ROWS, FOLD), jnp.bfloat16),
+            pltpu.VMEM((OBS, ROWS, 2 * W), f32),
             pltpu.VMEM((ACTIONS, W), f32),
             pltpu.VMEM((2, ROWS, W), f32),
             pltpu.VMEM((ROWS, ACTIONS * W), jnp.bfloat16),
@@ -348,7 +425,13 @@
             pltpu.VMEM((CHIPS, ROWS, W), f32),
             pltpu.VMEM((STEPS, CHIPS, ROWS, W), f32),
             pltpu.VMEM((STEPS, ROWS, W), f32),
+            pltpu.VMEM((ROWS, W), f32),
+            pltpu.VMEM((1, W), f32),
+            dma((SHARDS,)),
+            dma((2 * PLANES,)),
             dma((4,)),
+            dma((2 * PLANES,)),
+            dma,
             dma((SECTIONS,)),
             dma((SECTIONS,)),
             dma,

time: 125 us -> 118 us (0.944)
  Pallas kernels: 124 us -> 117 us
    pallas_call x1, Pallas kernels: 123 us -> 116 us  [local(): pl.pallas_call(kernel, out_shape=(jax.ShapeDtypeStruct((BELIEFS, W), f32)...]
where the time goes in v5:
time: 118 us
  Pallas kernels  117 us (99%)
    pallas_call x1, Pallas kernels, local(): pl.pallas_call(kernel, out_shape=(jax.ShapeDtypeStruct((BELIEFS, W), f32)...  116 us

profile of v5, /device:TPU:1, one launch (start us, length us, event | category | flops | bytes accessed | tf_op | source)
XLA Modules:
  0.0 118.0 jit_solution(1744131828140256435)
XLA Ops:
  0.6 115.6 %chain.1 = (f32[512,128]{1,0:T(8,128)}, f32[16,8,128]{2,1,0:T(8,128)}) custom-call(s32[32,512]{1,0:T(8,128)} %bitcast.9, s32[1,512]{1,0:T(1,128)} %action_ref.1, f32[8,128]{1,0:T(8,128)} %reward_ref.1, f32[8,32,128]{2,1,0:T(8,128)} %obs_hbm.1, f32[512,128]{1,0:T(8,128)} %terminal_hbm.1, bf16[1024,2048]{1,0:T(8,128)(2,1)} %bitcast.7, f32[512,128]{1,0:T(8,128)} %bitcast.8), custom_call_target="tpu_custom_call" | custom-call | tf_op jit(solution)/shard_map/chain/pallas_call | solution.py:402
  116.3 1.7 %finish.1 = (f32[512,128]{1,0:T(8,128)}, f32[4,128]{1,0:T(4,128)}) custom-call(f32[512,128]{1,0:T(8,128)} %get-tuple-element.6.final_ref, f32[16,8,128]{2,1,0:T(8,128)} %get-tuple-element.7.vbuf_ref), custom_call_target="tpu_custom_call" | custom-call | tf_op jit(solution)/shard_map/finish/pallas_call | solution.py:458

commit v6 on v5

--- a/solution.py
+++ b/solution.py
@@ -22,14 +22,15 @@
 FOLD = 256
 TAB = 40
 GROUP = 8
-GROUPS = ((0,), (1, 2), (3, 4), (5, 6, 7))
+GROUPS = ((0, 1), (2, 3, 4, 5), (6, 7))
 LAST = STEPS - 1
+DIRECT = 1
 
 
 def kernel(
-    next_ref, action_ref, reward_ref, obs_hbm, terminal_hbm, trans_hbm, belief_hbm,
+    next_hbm, action_hbm, reward_hbm, obs_hbm, terminal_hbm, trans_hbm, belief_hbm,
     final, vbuf,
-    obs, trans, belief, nbuf, tab, idx, turned, onehot, weight, reward, rewrow, masked,
+    next_ref, action_ref, reward_ref, obs, trans, belief, nbuf, tab, idx, turned, onehot, weight, reward, rewrow, masked,
     pair_send, pair_recv, part_send, part_recv, fresh,
     bel, vsend, own_ssem, own_rsem, load_sem, bel_ssem, bel_rsem, idx_ssem, idx_rsem, reward_ssem, reward_rsem, pair_ssem, pair_rsem, part_ssem, part_rsem,
     row_ssem, row_rsem, out_ssem, out_rsem, val_ssem, val_rsem,
@@ -64,7 +65,12 @@
         pltpu.make_async_copy(trans_hbm, trans, load_sem.at[2]),
         pltpu.make_async_copy(belief_hbm, belief, load_sem.at[3]),
     ]
-    for load in loads:
+    small = [
+        pltpu.make_async_copy(next_hbm, next_ref, load_sem.at[4]),
+        pltpu.make_async_copy(action_hbm, action_ref, load_sem.at[5]),
+        pltpu.make_async_copy(reward_hbm, reward_ref, load_sem.at[6]),
+    ]
+    for load in small:
         load.start()
 
     barrier = pltpu.get_barrier_semaphore()
@@ -75,6 +81,11 @@
     for up in (True, False):
         for d in range(PLANES):
             pl.semaphore_signal(barrier, inc=1, device_id=z_neighbour(up, d), device_id_type=MESH)
+
+    for load in loads:
+        load.start()
+    for load in small:
+        load.wait()
 
     for p in range(PLANES):
         tab[p, 0:OBS, :] = next_ref[:, p * BATCH : (p + 1) * BATCH]
@@ -157,6 +168,13 @@
             device_id={"section": sec, "state": chip_at(k, 0) * 2 + core}, device_id_type=MESH,
         )
 
+    def cross_copy(k, t):
+        return pltpu.make_async_remote_copy(
+            src_ref=pair_send.at[k], dst_ref=part_recv.at[t, CHIPS + k],
+            send_sem=pair_ssem.at[k], recv_sem=part_rsem.at[t, CHIPS + k],
+            device_id={"section": sec, "state": chip_at(k, 0) * 2 + 1 - core}, device_id_type=MESH,
+        )
+
     users = tuple((d, up) for d in range(PLANES) for up in (True, False))
 
     def row_copy(u, t):
@@ -253,8 +271,12 @@
                 pair_send[k] = jnp.where(core == 0, part[:, W:], part[:, :W])
                 part_send[k] = jnp.where(core == 0, part[:, :W], part[:, W:])
             for k in group:
-                pair_copy(k, t).start()
-        for k in range(CHIPS):
+                if k < DIRECT:
+                    part_copy(k, t).start()
+                    cross_copy(k, t).start()
+                else:
+                    pair_copy(k, t).start()
+        for k in range(DIRECT, CHIPS):
             pair_copy(k, t).wait_recv()
             part_send[k] = part_send[k] + pair_recv[t, k]
             if k < CHIPS - 1:
@@ -268,9 +290,14 @@
         def _():
             prepare(t + 1)
 
-        for k in range(CHIPS):
+        for k in range(DIRECT):
+            cross_copy(k, t).wait_send()
+        for k in range(DIRECT, CHIPS):
             pair_copy(k, t).wait_send()
         summed = part_send[CHIPS - 1]
+        for k in range(DIRECT):
+            cross_copy(k, t).wait_recv()
+            summed = summed + part_recv[t, CHIPS + k]
         for k in range(CHIPS - 1):
             part_copy(k, t).wait_recv()
             summed = summed + part_recv[t, k]
@@ -385,13 +412,15 @@
             val_copy(d).wait_send()
 
 
-def finish(final_ref, vbuf_ref, alphas_ref, values_ref):
-    alphas_ref[...] = final_ref[...]
+def finish(final_ref, vbuf_ref, alphas_hbm, values_ref, sem):
+    out = pltpu.make_async_copy(final_ref, alphas_hbm, sem)
+    out.start()
     value = vbuf_ref[0]
     for s in range(1, SHARDS):
         value = value + vbuf_ref[s]
     for p in range(PLANES):
         values_ref[p : p + 1, :] = value[2 * p : 2 * p + 1, :] + value[2 * p + 1 : 2 * p + 2, :]
+    out.wait()
 
 
 def local(belief, action, next_index, obs_table, transition, reward, terminal):
@@ -402,12 +431,15 @@
     final, parts = pl.pallas_call(
         kernel,
         out_shape=(
-            jax.ShapeDtypeStruct((BELIEFS, W), f32),
-            jax.ShapeDtypeStruct((SHARDS, 2 * PLANES, W), f32),
+            pltpu.VMEM((BELIEFS, W), f32),
+            pltpu.VMEM((SHARDS, 2 * PLANES, W), f32),
         ),
-        in_specs=[vmem, vmem, vmem, anywhere, anywhere, anywhere, anywhere],
+        in_specs=[anywhere] * 7,
         out_specs=(vmem, vmem),
         scratch_shapes=[
+            pltpu.VMEM((OBS, BELIEFS), jnp.int32),
+            pltpu.VMEM((1, BELIEFS), jnp.int32),
+            pltpu.VMEM((ACTIONS, W), f32),
             pltpu.VMEM((ACTIONS, OBS, W), f32),
             pltpu.VMEM((ACTIONS * W, SHARDS * W), jnp.bfloat16),
             pltpu.VMEM((BELIEFS, W), f32),
@@ -423,13 +455,13 @@
             pltpu.VMEM((CHIPS, ROWS, W), f32),
             pltpu.VMEM((STEPS, CHIPS, ROWS, W), f32),
             pltpu.VMEM((CHIPS, ROWS, W), f32),
-            pltpu.VMEM((STEPS, CHIPS, ROWS, W), f32),
+            pltpu.VMEM((STEPS, CHIPS + DIRECT, ROWS, W), f32),
             pltpu.VMEM((STEPS, ROWS, W), f32),
             pltpu.VMEM((ROWS, W), f32),
             pltpu.VMEM((1, W), f32),
             dma((SHARDS,)),
             dma((2 * PLANES,)),
-            dma((4,)),
+            dma((7,)),
             dma((2 * PLANES,)),
             dma,
             dma((SECTIONS,)),
@@ -439,7 +471,7 @@
             dma((CHIPS,)),
             dma((STEPS, CHIPS)),
             dma((CHIPS,)),
-            dma((STEPS, CHIPS)),
+            dma((STEPS, CHIPS + DIRECT)),
             dma((2 * PLANES,)),
             dma((STEPS, 2 * PLANES)),
             dma,
@@ -462,9 +494,13 @@
             jax.ShapeDtypeStruct((PLANES, W), f32),
         ),
         in_specs=[vmem, vmem],
-        out_specs=(vmem, vmem),
+        out_specs=(anywhere, vmem),
+        scratch_shapes=[dma],
         name="finish",
-    )(final, parts)
+    )(
+        pltpu.with_memory_space_constraint(final, pltpu.VMEM),
+        pltpu.with_memory_space_constraint(parts, pltpu.VMEM),
+    )
     return alphas[None], values.reshape(1, BELIEFS)
 
 

time: 118 us -> 115 us (0.975)
  Pallas kernels: 117 us -> 115 us
    pallas_call x1, Pallas kernels: 116 us -> 113 us  [local(): pl.pallas_call(kernel, out_shape=(pltpu.VMEM((BELIEFS, W), f32), pltpu.VM...]
where the time goes in v6:
time: 115 us
  Pallas kernels  115 us (100%)
    pallas_call x1, Pallas kernels, local(): pl.pallas_call(kernel, out_shape=(pltpu.VMEM((BELIEFS, W), f32), pltpu.VM...  113 us

profile of v6, /device:TPU:1, one launch (start us, length us, event | category | flops | bytes accessed | tf_op | source)
XLA Modules:
  0.0 115.3 jit_solution(14513264708153858379)
XLA Ops:
  0.6 113.4 %chain.1 = (f32[512,128]{1,0:T(8,128)S(1)}, f32[16,8,128]{2,1,0:T(8,128)S(1)}) custom-call(s32[32,512]{1,0:T(8,128)} %bitcast.9, s32[1,512]{1,0:T(1,128)} %action_hbm.1, f32[8,128]{1,0:T(8,128)} %reward_hbm.1, f32[8,32,128]{2,1,0:T(8,128)} %obs_hbm.1, f32[512,128]{1,0:T(8,128)} %terminal_hbm.1, bf16[1024,2048]{1,0:T(8,128)(2,1)} %bitcast.7, f32[512,128]{1,0:T(8,128)} %bitcast.8), custom_call_target="tpu_custom_call" | custom-call | tf_op jit(solution)/shard_map/chain/pallas_call | solution.py:431
  114.0 1.3 %finish.1 = (f32[512,128]{1,0:T(8,128)}, f32[4,128]{1,0:T(4,128)}) custom-call(f32[512,128]{1,0:T(8,128)S(1)} %get-tuple-element.6.final_ref, f32[16,8,128]{2,1,0:T(8,128)S(1)} %get-tuple-element.7.vbuf_ref), custom_call_target="tpu_custom_call" | custom-call | tf_op jit(solution)/shard_map/finish/pallas_call | solution.py:490

commit v7 on v6

--- a/solution.py
+++ b/solution.py
@@ -24,6 +24,7 @@
 GROUP = 8
 GROUPS = ((0, 1), (2, 3, 4, 5), (6, 7))
 LAST = STEPS - 1
+OWN = 2 * (PLANES - 1)
 DIRECT = 1
 
 
@@ -37,7 +38,7 @@
 ):
     sec = lax.axis_index("section")
     st = lax.axis_index("state")
-    plane, half = lax.rem(sec, PLANES), lax.div(sec, PLANES)
+    plane, half = PLANES - 1 - lax.rem(sec, PLANES), lax.div(sec, PLANES)
     core, chip = lax.rem(st, 2), lax.div(st, 2)
     lo, y = lax.div(chip, 4), lax.rem(chip, 4)
 
@@ -55,7 +56,7 @@
     def z_neighbour(up, d):
         z = lax.rem(half * 2 + lo + (1 if up else 3), 4)
         return {
-            "section": lax.div(z, 2) * PLANES + lax.rem(plane + d, PLANES),
+            "section": lax.div(z, 2) * PLANES + PLANES - 1 - lax.rem(plane + d, PLANES),
             "state": (lax.rem(z, 2) * 4 + y) * 2 + core,
         }
 
@@ -102,14 +103,14 @@
     def idx_copy(d):
         to = other_section(d)
         return pltpu.make_async_remote_copy(
-            src_ref=tab.at[lax.rem(to, PLANES)], dst_ref=idx.at[sec],
+            src_ref=tab.at[PLANES - 1 - lax.rem(to, PLANES)], dst_ref=idx.at[sec],
             send_sem=idx_ssem.at[d], recv_sem=idx_rsem.at[sec],
             device_id={"section": to, "state": st}, device_id_type=MESH,
         )
 
     @pl.when(sec == SECTIONS - 1)
     def _():
-        for d in (1, 5, 2, 6, 3, 7, 4):
+        for d in (4, 7, 3, 6, 2, 5, 1):
             idx_copy(d).start()
 
     reward_copy = pltpu.make_async_remote_copy(
@@ -175,7 +176,7 @@
             device_id={"section": sec, "state": chip_at(k, 0) * 2 + 1 - core}, device_id_type=MESH,
         )
 
-    users = tuple((d, up) for d in range(PLANES) for up in (True, False))
+    users = tuple((d, up) for d in (1, 0, 3, 2) for up in (True, False))
 
     def row_copy(u, t):
         d, up = users[u]
@@ -197,13 +198,13 @@
         )
 
     def goes_out(t):
-        return (lax.rem(STEPS - 1 - t, PLANES) < plane) | (t == STEPS - 1)
+        return (PLANES - 1 - lax.rem(STEPS - 1 - t, PLANES) < plane) | (t == STEPS - 1)
 
     def bel_copy(m):
         return pltpu.make_async_remote_copy(
             src_ref=belief.at[m * ROWS : (m + 1) * ROWS], dst_ref=bel,
             send_sem=bel_ssem.at[m], recv_sem=bel_rsem,
-            device_id={"section": (m % 2) * PLANES + m // 2, "state": ((1 - lo) * 4 + y) * 2 + core},
+            device_id={"section": (m % 2) * PLANES + PLANES - 1 - m // 2, "state": ((1 - lo) * 4 + y) * 2 + core},
             device_id_type=MESH,
         )
 
@@ -311,7 +312,7 @@
         def _():
             out_copy(t).start()
 
-        @pl.when((t == LAST - 2) & (sec == 0))
+        @pl.when((t == 1) & (sec == 0))
         def _():
             loads[3].wait()
             for m in range(2 * PLANES):
@@ -381,9 +382,9 @@
 
     @pl.when(sec == 0)
     def _():
-        vbuf[pl.ds(st, 1), 0:1, :] = vsend[...][None]
+        vbuf[pl.ds(st, 1), OWN : OWN + 1, :] = vsend[...][None]
         for m in range(2 * PLANES):
-            count = SHARDS if m else SHARDS - 1
+            count = SHARDS - 1 if m == OWN else SHARDS
             pltpu.make_async_remote_copy(
                 src_ref=vbuf.at[pl.ds(0, count), m], dst_ref=vbuf.at[pl.ds(0, count), m],
                 send_sem=own_ssem.at[0], recv_sem=own_rsem.at[m],
@@ -412,15 +413,13 @@
             val_copy(d).wait_send()
 
 
-def finish(final_ref, vbuf_ref, alphas_hbm, values_ref, sem):
-    out = pltpu.make_async_copy(final_ref, alphas_hbm, sem)
-    out.start()
+def finish(final_ref, vbuf_ref, alphas_ref, values_ref):
+    alphas_ref[...] = final_ref[...]
     value = vbuf_ref[0]
     for s in range(1, SHARDS):
         value = value + vbuf_ref[s]
     for p in range(PLANES):
         values_ref[p : p + 1, :] = value[2 * p : 2 * p + 1, :] + value[2 * p + 1 : 2 * p + 2, :]
-    out.wait()
 
 
 def local(belief, action, next_index, obs_table, transition, reward, terminal):
@@ -494,8 +493,7 @@
             jax.ShapeDtypeStruct((PLANES, W), f32),
         ),
         in_specs=[vmem, vmem],
-        out_specs=(anywhere, vmem),
-        scratch_shapes=[dma],
+        out_specs=(vmem, vmem),
         name="finish",
     )(
         pltpu.with_memory_space_constraint(final, pltpu.VMEM),

time: 115 us -> 113 us (0.983)
  Pallas kernels: 115 us -> 112 us
    pallas_call x1, Pallas kernels: 113 us -> 111 us  [local(): pl.pallas_call(kernel, out_shape=(pltpu.VMEM((BELIEFS, W), f32), pltpu.VM...]
where the time goes in v7:
time: 113 us
  Pallas kernels  112 us (99%)
    pallas_call x1, Pallas kernels, local(): pl.pallas_call(kernel, out_shape=(pltpu.VMEM((BELIEFS, W), f32), pltpu.VM...  111 us

profile of v7, /device:TPU:1, one launch (start us, length us, event | category | flops | bytes accessed | tf_op | source)
XLA Modules:
  0.0 112.8 jit_solution(6533610794783232998)
XLA Ops:
  0.6 111.5 %chain.1 = (f32[512,128]{1,0:T(8,128)S(1)}, f32[16,8,128]{2,1,0:T(8,128)S(1)}) custom-call(s32[32,512]{1,0:T(8,128)} %bitcast.9, s32[1,512]{1,0:T(1,128)} %action_hbm.1, f32[8,128]{1,0:T(8,128)} %reward_hbm.1, f32[8,32,128]{2,1,0:T(8,128)} %obs_hbm.1, f32[512,128]{1,0:T(8,128)} %terminal_hbm.1, bf16[1024,2048]{1,0:T(8,128)(2,1)} %bitcast.7, f32[512,128]{1,0:T(8,128)} %bitcast.8), custom_call_target="tpu_custom_call" | custom-call | tf_op jit(solution)/shard_map/chain/pallas_call | solution.py:430
  112.1 0.7 finish.1

commit v8 on v7

--- a/solution.py
+++ b/solution.py
@@ -150,7 +150,7 @@
             weight[o, :, :W] = jnp.where(upper, 0.0, w)
             weight[o, :, W:] = jnp.where(upper, w, 0.0)
 
-    order = ((1, 2), (0, 2), (1, 1), (1, 3), (0, 1), (0, 3), (1, 0), (0, 0))
+    order = ((1, 2), (1, 1), (1, 3), (0, 2), (1, 0), (0, 1), (0, 3), (0, 0))
 
     def chip_at(k, flip):
         return lax.rem(lo + order[k][0] + flip, 2) * 4 + lax.rem(y + order[k][1], 4)

time: 113 us -> 112 us (level)
  no operation moved by 1% of the time
where the time goes in v8:
time: 112 us
  Pallas kernels  111 us (99%)
    pallas_call x1, Pallas kernels, local(): pl.pallas_call(kernel, out_shape=(pltpu.VMEM((BELIEFS, W), f32), pltpu.VM...  111 us

profile of v8, /device:TPU:1, one launch (start us, length us, event | category | flops | bytes accessed | tf_op | source)
XLA Modules:
  0.0 112.0 jit_solution(10086250842154833203)
XLA Ops:
  0.6 110.6 %chain.1 = (f32[512,128]{1,0:T(8,128)S(1)}, f32[16,8,128]{2,1,0:T(8,128)S(1)}) custom-call(s32[32,512]{1,0:T(8,128)} %bitcast.9, s32[1,512]{1,0:T(1,128)} %action_hbm.1, f32[8,128]{1,0:T(8,128)} %reward_hbm.1, f32[8,32,128]{2,1,0:T(8,128)} %obs_hbm.1, f32[512,128]{1,0:T(8,128)} %terminal_hbm.1, bf16[1024,2048]{1,0:T(8,128)(2,1)} %bitcast.7, f32[512,128]{1,0:T(8,128)} %bitcast.8), custom_call_target="tpu_custom_call" | custom-call | tf_op jit(solution)/shard_map/chain/pallas_call | solution.py:430
  111.2 0.7 finish.1

commit v9 on v8

--- a/solution.py
+++ b/solution.py
@@ -150,7 +150,7 @@
             weight[o, :, :W] = jnp.where(upper, 0.0, w)
             weight[o, :, W:] = jnp.where(upper, w, 0.0)
 
-    order = ((1, 2), (1, 1), (1, 3), (0, 2), (1, 0), (0, 1), (0, 3), (0, 0))
+    order = ((1, 2), (1, 0), (1, 1), (1, 3), (0, 2), (0, 1), (0, 3), (0, 0))
 
     def chip_at(k, flip):
         return lax.rem(lo + order[k][0] + flip, 2) * 4 + lax.rem(y + order[k][1], 4)

time: 112 us -> 111 us (level)
    pallas_call x1, Pallas kernels: 111 us -> 109 us  [local(): pl.pallas_call(kernel, out_shape=(pltpu.VMEM((BELIEFS, W), f32), pltpu.VM...]
where the time goes in v9:
time: 111 us
  Pallas kernels  110 us (99%)
    pallas_call x1, Pallas kernels, local(): pl.pallas_call(kernel, out_shape=(pltpu.VMEM((BELIEFS, W), f32), pltpu.VM...  109 us

profile of v9, /device:TPU:1, one launch (start us, length us, event | category | flops | bytes accessed | tf_op | source)
XLA Modules:
  0.0 110.8 jit_solution(226854514374363702)
XLA Ops:
  0.6 109.4 %chain.1 = (f32[512,128]{1,0:T(8,128)S(1)}, f32[16,8,128]{2,1,0:T(8,128)S(1)}) custom-call(s32[32,512]{1,0:T(8,128)} %bitcast.9, s32[1,512]{1,0:T(1,128)} %action_hbm.1, f32[8,128]{1,0:T(8,128)} %reward_hbm.1, f32[8,32,128]{2,1,0:T(8,128)} %obs_hbm.1, f32[512,128]{1,0:T(8,128)} %terminal_hbm.1, bf16[1024,2048]{1,0:T(8,128)(2,1)} %bitcast.7, f32[512,128]{1,0:T(8,128)} %bitcast.8), custom_call_target="tpu_custom_call" | custom-call | tf_op jit(solution)/shard_map/chain/pallas_call | solution.py:430
  110.1 0.7 finish.1
